TPU v7x, 32 devices: a whole 2x2x4 slice. The times are simulated.
32 devices in a mesh: front: 8 (over z, x), panel: 4 (over y, core).
Axes of the slice: x: 2, y: 2, z: 4, core: 2. Of those that a mesh axis runs over, the one named last changes fastest.
Arguments:
- coupling: bfloat16 [8, 2048, 2048], P('front', 'panel'), may hold values from -1 to 1
- pivot_inverse: bfloat16 [8, 2048, 2048], P('front', 'panel'), may hold values from -0.125 to 0.125
- pivots: float32 [8, 2048], P('front'), as said below
- trailing: float32 [8, 2048, 2048], P('front', 'panel'), may hold values from -12 to 12
- sketch: float32 [8, 8, 8, 32, 256], P('front', 'panel'), may hold values from -6 to 6
- extend_map: int32 [8, 2048], replicated, may hold values from 0 to 1023, as said below
- parent_of: int32 [8], replicated, may hold values from 0 to 7, as said below
- parent_base: bfloat16 [8, 4096, 4096], P('front', 'panel'), may hold values from -6 to 6
Outputs:
- assembled: bfloat16 [8, 4096, 4096], P('front', 'panel')
Inputs may be any that keep to these rules, and one draw needn't show every extreme that they name: `extend_map`: within each front and each aligned block of 2048 / 4 entries the values are distinct and rising. `pivots`: every entry's magnitude lies between 0.5 and 2 times 2048 ** -0.5; signs are mixed. `parent_of`: no parent has more than 4 children; some parent has exactly 4.
All inputs are finite; a program needn't handle non-finite values.
Results may differ from a plain program's by a relative error of at most 0.0043.
Values may be sent and summed in bfloat16 or wider, within the bound.
No kernel may reach another device: no remote copies, remote signals or barrier semaphores. Data moves between devices by JAX's collectives and lax.ppermute only.
A program may use at most 128 MiB of HBM per device.

v0:
```python
import functools

import jax
import jax.numpy as jnp
from jax import lax
from jax.experimental import pallas as pl
from jax.experimental.pallas import tpu as pltpu
from jax.sharding import PartitionSpec as P


KIDS = 4
NT = (((1,), (1,)), ((), ()))
NN = (((1,), (0,)), ((), ()))


VMEM = pl.BlockSpec(memory_space=pltpu.VMEM)
SMEM = pl.BlockSpec(memory_space=pltpu.SMEM)
HBM = pl.BlockSpec(memory_space=pltpu.HBM)


def in_hbm(arrays):
    return [pltpu.with_memory_space_constraint(x, pltpu.HBM) for x in arrays]


def mm(a, b, dims):
    return lax.dot_general(a, b, dims, preferred_element_type=jnp.float32)


def halves(x):
    high = x.astype(jnp.bfloat16)
    return high, (x - high.astype(jnp.float32)).astype(jnp.bfloat16)


def dot3(a, b, dims):
    a_hi, a_lo = a
    b_hi, b_lo = b
    rows = a_hi.shape[0]
    both = mm(jnp.concatenate([a_hi, a_lo], axis=0), b_hi, dims)
    return both[:rows] + (mm(a_hi, b_lo, dims) + both[rows:])


def swap(x, axis, bit):
    return lax.ppermute(x, axis, [(s, s ^ bit) for s in range(lax.axis_size(axis))])


def bits_of(count, lowest):
    bits = []
    bit = count // 2
    while bit >= lowest:
        bits.append(bit)
        bit //= 2
    return bits


def factor_kernel(meta, coupling, pivots, *refs, first):
    *inverses, factor, scaled = refs
    width = factor.shape[1]
    total = None
    for n, inverse in enumerate(inverses):
        rows = inverse.shape[0]
        at = pl.multiple_of(meta[n] * rows, rows)
        lo = first if inverse.shape[1] > width else 0
        term = mm(coupling[:, pl.ds(at, rows)], inverse[:, lo:lo + width], NN)
        total = term if total is None else total + term
    rounded = total.astype(jnp.bfloat16)
    factor[...] = rounded
    scaled[...] = (rounded.astype(jnp.float32) / pivots[:, first:first + width]).astype(jnp.bfloat16)


def factor_columns(meta, coupling, pivots, inverses, first, width):
    rows = coupling.shape[0]
    out = jax.ShapeDtypeStruct((rows, width), jnp.bfloat16)
    return pl.pallas_call(
        functools.partial(factor_kernel, first=first),
        in_specs=[SMEM] + [VMEM] * (2 + len(inverses)),
        out_specs=[VMEM, VMEM],
        out_shape=[out, out],
        compiler_params=pltpu.CompilerParams(vmem_limit_bytes=32 << 20),
        cost_estimate=pl.CostEstimate(
            flops=2 * rows * coupling.shape[1] * out.shape[1], transcendentals=0, bytes_accessed=1 << 22
        ),
        name="factor",
    )(meta, coupling, pivots, *inverses)


def compress_kernel(meta, *refs, pieces, choices):
    count = len(pieces)
    scaled_a, scaled_b, trailing, omega = refs[:4]
    firsts = []
    at = 4
    for n in range(count):
        firsts.append(refs[at:at + choices[n]])
        at += choices[n]
    seconds = refs[at:at + count]
    out, left_a, left_b = refs[at + count:at + count + 3]
    local = refs[at + count + 3:at + count + 3 + 4 * count]
    tiles, ranges, grams, sems = refs[at + count + 3 + 4 * count:]
    tile_rows, rank, size = omega.shape[0], omega.shape[2], omega.shape[3]
    batch = sum(pieces) * tile_rows

    def copies(n, which):
        first, second, old, draws = local[4 * n:4 * n + 4]
        start = pl.multiple_of(meta[4 * n] * size, size)
        column = meta[4 * n + 1]
        left = pl.multiple_of(column * size, size)
        span = pieces[n] * size
        sem = 2 + 4 * n
        source, target = (
            (lambda x: firsts[n][x].at[pl.ds(start, span)], first),
            (lambda x: seconds[n], second),
            (lambda x: trailing.at[:, pl.ds(left, span)], old),
            (lambda x: omega.at[:, pl.ds(column, pieces[n])], draws),
        )[which]
        return lambda x=0: pltpu.make_async_copy(source(x), target, sems.at[sem + which])

    def start_copies(n, which):
        make = copies(n, which)
        if which > 0 or choices[n] == 1:
            make().start()
        else:
            for x in range(choices[n]):
                @pl.when(meta[4 * n + 3] == x)
                def _():
                    make(x).start()

    scaled_copies = (
        pltpu.make_async_copy(scaled_a, left_a, sems.at[0]),
        pltpu.make_async_copy(scaled_b, left_b, sems.at[1]),
    )
    scaled_copies[0].start()
    start_copies(0, 0)
    scaled_copies[1].start()
    for n in range(count):
        for which in range(4):
            if n > 0 or which > 0:
                start_copies(n, which)

    at = 0
    for n in range(count):
        first, second, old, draws = local[4 * n:4 * n + 4]
        if n == 0:
            scaled_copies[0].wait()
        copies(n, 0)().wait()
        update = mm(left_a[...], first[...], NT)
        if n == 0:
            scaled_copies[1].wait()
        copies(n, 1)().wait()
        update = update + mm(left_b[...], second[...], NT)
        copies(n, 2)().wait()
        schur = old[...] - update
        copies(n, 3)().wait()
        for t in range(pieces[n]):
            for i in range(tile_rows):
                tile = schur[i * size:(i + 1) * size, t * size:(t + 1) * size]
                tiles[at] = tile
                y = dot3(halves(draws[i, t]), halves(tile), NT)
                ranges[at] = y
                grams[at] = lax.dot_general(
                    y, y, NT, precision=lax.Precision.HIGHEST, preferred_element_type=jnp.float32
                )
                at += 1
    row_id = lax.broadcasted_iota(jnp.int32, (batch, rank, rank), 1)
    col_id = lax.broadcasted_iota(jnp.int32, (batch, rank, rank), 2)
    eye = jnp.where(row_id == col_id, 1.0, 0.0).astype(jnp.float32)
    work = jnp.concatenate([grams[...], eye], axis=2)
    rows = lax.broadcasted_iota(jnp.int32, (batch, rank, 1), 1)
    for k in range(rank):
        scale = lax.rsqrt(work[:, k:k + 1, k:k + 1])
        pivot_row = work[:, k:k + 1, :] * scale
        column = work[:, :, k:k + 1] * scale
        below = jnp.where(rows > k, column, 0.0)
        work = jnp.where(rows == k, pivot_row, work - below * pivot_row)
    inverse = work[:, :, rank:]
    at = 0
    for n in range(count):
        for t in range(pieces[n]):
            slot = meta[4 * n + 2] + t
            for i in range(tile_rows):
                u = lax.dot_general(
                    inverse[at], ranges[at], NN,
                    precision=lax.Precision.HIGHEST, preferred_element_type=jnp.float32,
                )
                out[0, i, slot] = u.astype(jnp.bfloat16)
                out[1, i, slot] = dot3(halves(u), halves(tiles[at]), NN).astype(jnp.bfloat16)
                at += 1


def compress(scaled, trailing, omega, parts):
    tile_rows, _, rank, size = omega.shape
    rows, width = trailing.shape
    pieces = tuple(part[3].shape[0] // size for part in parts)
    choices = tuple(len(part[0]) for part in parts)
    total = sum(pieces)
    meta = jnp.stack(
        [jnp.int32(0) + x for part in parts for x in (part[2], part[4], part[5], part[1])]
    ).astype(jnp.int32)
    out = jax.ShapeDtypeStruct((2, tile_rows, total, rank, size), jnp.bfloat16)
    batch = total * tile_rows
    operands = [*scaled, trailing, omega]
    local = []
    for part, piece in zip(parts, pieces):
        operands += part[0]
        local += [
            pltpu.VMEM((piece * size, part[0][0].shape[1]), jnp.bfloat16),
            pltpu.VMEM(part[3].shape, jnp.bfloat16),
            pltpu.VMEM((rows, piece * size), jnp.float32),
            pltpu.VMEM((tile_rows, piece, rank, size), jnp.float32),
        ]
    operands += [part[3] for part in parts]
    return pl.pallas_call(
        functools.partial(compress_kernel, pieces=pieces, choices=choices),
        in_specs=[SMEM] + [HBM] * len(operands),
        out_specs=VMEM,
        out_shape=out,
        scratch_shapes=[pltpu.VMEM(x.shape, jnp.bfloat16) for x in scaled] + local + [
            pltpu.VMEM((batch, size, size), jnp.float32),
            pltpu.VMEM((batch, rank, size), jnp.float32),
            pltpu.VMEM((batch, rank, rank), jnp.float32),
            pltpu.SemaphoreType.DMA((2 + 4 * len(parts),)),
        ],
        compiler_params=pltpu.CompilerParams(vmem_limit_bytes=40 << 20),
        cost_estimate=pl.CostEstimate(
            flops=8 * rows * width * total * size, transcendentals=0, bytes_accessed=8 * rows * width
        ),
        name="compress",
    )(meta, *in_hbm(operands))


def place_kernel(meta, maps, base, *refs, fronts, blocks, row_dev):
    count = len(blocks)
    packs = [refs[n * fronts:(n + 1) * fronts] for n in range(count)]
    out, *mine = refs[-(5 + count):-4]
    lines, left, right, sems = refs[-4:]
    _, tile_rows, _, rank, size = packs[0][0].shape
    steps, height, width = lines.shape
    per_block = row_dev // size
    group = per_block * rank
    depth = tile_rows * group
    spare = height - row_dev

    def fetch(n, slot, go):
        for offset in range(fronts):
            @pl.when(jnp.logical_and(meta[slot] >= 0, meta[KIDS + slot] == offset))
            def _():
                go(pltpu.make_async_copy(packs[n][offset], mine[n].at[slot], sems.at[n * KIDS + slot]))

    def columns(step):
        return pl.ds(pl.multiple_of(meta[2 * KIDS + 1 + step] * width, width), width)

    def load(step):
        return pltpu.make_async_copy(base.at[:, columns(step)], lines.at[step], sems.at[count * KIDS + step])

    def store(step):
        return pltpu.make_async_copy(lines.at[step], out.at[:, columns(step)], sems.at[count * KIDS + steps + step])

    def selection(panel, child, t):
        lane = pl.multiple_of(panel * row_dev + t * size, size)
        ids = maps[pl.ds(child, 1), pl.ds(lane, size)] - t * size
        hit = lax.broadcasted_iota(jnp.int32, (size + spare, size), 0) == ids
        return jnp.where(hit, 1.0, 0.0).astype(jnp.bfloat16)

    for n in range(count):
        for slot in range(KIDS):
            fetch(n, slot, lambda copy: copy.start())
    for step in range(steps):
        load(step).start()
    left[...] = jnp.zeros(left.shape, left.dtype)
    right[...] = jnp.zeros(right.shape, right.dtype)
    for n in range(count):
        for slot in range(KIDS):
            fetch(n, slot, lambda copy: copy.wait())
    for slot in range(KIDS):
        lo = slot * depth

        @pl.when(meta[slot] >= 0)
        def _():
            for i in range(tile_rows):
                source = jnp.concatenate(
                    [mine[n][slot, 0, i].reshape(blocks[n] * group, size) for n in range(count)], axis=0
                )
                spread = mm(selection(meta[2 * KIDS], meta[slot], i), source, NT).astype(jnp.bfloat16)
                for step in range(steps):
                    left[step, i * size:(i + 1) * size + spare, lo + i * group:lo + (i + 1) * group] = (
                        spread[:, step * group:(step + 1) * group]
                    )

    step = 0
    for n in range(count):
        for b in range(blocks[n]):
            for slot in range(KIDS):
                lo = slot * depth

                @pl.when(meta[slot] >= 0)
                def _():
                    for t in range(per_block):
                        source = jnp.concatenate(
                            [mine[n][slot, 1, i, b * per_block + t] for i in range(tile_rows)], axis=0
                        )
                        pick = selection(meta[2 * KIDS + 1 + step], meta[slot], t)
                        spread = mm(pick, source, NT).astype(jnp.bfloat16)
                        for i in range(tile_rows):
                            at = lo + i * group + t * rank
                            right[t * size:(t + 1) * size + spare, at:at + rank] = (
                                spread[:, i * rank:(i + 1) * rank]
                            )

            load(step).wait()
            lines[step] = (
                lines[step].astype(jnp.float32) + mm(left[step], right[...], NT)
            ).astype(jnp.bfloat16)
            store(step).start()
            step += 1
    for step in range(steps):
        store(step).wait()


def place(meta, extend_map, packs, base, row_dev, blocks, previous):
    fronts = len(packs[0])
    _, tile_rows, _, rank, size = packs[0][0].shape
    height, full = base.shape
    panels = extend_map.shape[1] // row_dev
    width = full // panels
    depth = KIDS * tile_rows * (row_dev // size) * rank
    steps = sum(blocks)
    operands = [base] + [x for chunk in packs for x in chunk]
    aliases = {}
    if previous is not None:
        operands.append(previous)
        aliases = {1 + len(operands): 0}
    return pl.pallas_call(
        functools.partial(place_kernel, fronts=fronts, blocks=blocks, row_dev=row_dev),
        in_specs=[SMEM, VMEM] + [HBM] * len(operands),
        out_specs=HBM,
        out_shape=jax.ShapeDtypeStruct(base.shape, base.dtype),
        scratch_shapes=[pltpu.VMEM((KIDS,) + chunk[0].shape, jnp.bfloat16) for chunk in packs] + [
            pltpu.VMEM((steps, height, width), jnp.bfloat16),
            pltpu.VMEM((steps, height, depth), jnp.bfloat16),
            pltpu.VMEM((width, depth), jnp.bfloat16),
            pltpu.SemaphoreType.DMA((len(packs) * KIDS + 2 * steps,)),
        ],
        input_output_aliases=aliases,
        compiler_params=pltpu.CompilerParams(vmem_limit_bytes=48 << 20),
        cost_estimate=pl.CostEstimate(
            flops=8 * height * width * steps * depth, transcendentals=0, bytes_accessed=4 * height * width * steps
        ),
        name="place",
    )(meta, extend_map, *in_hbm(operands))


def spread_panels(x, lowest):
    held = {0: x}
    for bit in bits_of(lax.axis_size("panel"), lowest):
        for offset in list(held):
            held[offset ^ bit] = swap(held[offset], "panel", bit)
    return held


def gather_fronts(pack):
    held = {0: pack}
    for bit in bits_of(lax.axis_size("front"), 1):
        for offset in list(held):
            held[offset ^ bit] = swap(held[offset], "front", bit)
    return [held[offset] for offset in range(len(held))]


def body(coupling, pivot_inverse, pivots, trailing, sketch, extend_map, parent_of, parent_base):
    rows_here = coupling[0]
    inverse = pivot_inverse[0]
    row_dev, width = rows_here.shape
    omega = sketch[0]
    size = omega.shape[3]
    panels = lax.axis_size("panel")
    panel_here = lax.axis_index("panel").astype(jnp.int32)
    owner = lax.axis_index("front").astype(jnp.int32)
    core = panel_here & 1
    per_block = row_dev // size
    middle = inverse.shape[1] // 2

    near_inverse = swap(inverse, "panel", 1)
    held_a = spread_panels(inverse[:, :middle], 2)
    held_b = spread_panels(lax.optimization_barrier(inverse)[:, middle:], 2)
    offsets = range(panels)
    panel_of = jnp.stack([panel_here ^ offset for offset in offsets])

    def columns(held, lo, hi):
        parts = []
        for offset in offsets:
            if offset == 0:
                parts.append(inverse)
            elif offset == 1:
                parts.append(near_inverse)
            elif offset & 1:
                parts.append(swap(held[offset ^ 1], "panel", 1))
            else:
                parts.append(held[offset])
        return factor_columns(panel_of, rows_here, pivots, parts, lo, hi - lo)

    factor_a, scaled_a = columns(held_a, 0, middle)
    far_a = spread_panels(factor_a, 2)
    near_a = {offset ^ 1: swap(x, "panel", 1) for offset, x in far_a.items()}
    first = {**far_a, **near_a}
    factor_b, scaled_b = columns(held_b, middle, width)
    near_b = swap(factor_b, "panel", 1)
    scaled = (scaled_a, scaled_b)

    fronts = parent_of.shape[0]
    mine = parent_of == owner
    rank_of = jnp.cumsum(mine.astype(jnp.int32)) - 1
    slots = jnp.arange(KIDS, dtype=jnp.int32)
    match = mine[None, :] & (rank_of[None, :] == slots[:, None])
    child = jnp.sum(jnp.where(match, jnp.arange(fronts, dtype=jnp.int32)[None, :] + 1, 0), axis=1) - 1
    slot_meta = jnp.concatenate([child, jnp.maximum(child, 0) ^ owner, panel_here[None]]).astype(jnp.int32)

    mate = panel_here ^ 1
    chunks = [(
        [panel_here, mate],
        [
            ([factor_a], 0, 0, factor_b, panel_here * per_block, 0),
            ([first[1]], 0, 0, near_b, mate * per_block, per_block),
        ],
    )]
    if per_block % 2 == 0:
        half = row_dev // 2
        tiles = per_block // 2
        pieces = []
        for c in range(2):
            chosen = jnp.where(
                core == c,
                lax.dynamic_slice_in_dim(factor_b, core * half, half, 0),
                lax.dynamic_slice_in_dim(near_b, core * half, half, 0),
            )
            pieces.append(spread_panels(chosen, 2))
        for offset in sorted(pieces[0])[1:]:
            for c in range(2):
                here = pieces[c][offset]
                there = swap(here, "panel", 1)
                block = ((panel_here ^ offset) & ~1) + c
                both = [first[offset], first[offset ^ 1]]
                parts = [
                    (both, core ^ c, x * tiles, piece, block * per_block + x * tiles, x * tiles)
                    for x, piece in ((core, here), (1 - core, there))
                ]
                chunks.append(([block], parts))
    else:
        held = spread_panels(factor_b, 2)
        for offset in sorted(held)[1:]:
            block = panel_here ^ offset
            there = swap(held[offset], "panel", 1)
            chunks.append((
                [block, block ^ 1],
                [
                    ([first[offset]], 0, 0, held[offset], block * per_block, 0),
                    ([first[offset ^ 1]], 0, 0, there, (block ^ 1) * per_block, per_block),
                ],
            ))

    packs = []
    for _, parts in chunks:
        packs.append(compress(scaled, trailing[0], omega, parts))
    gathered = []
    for pack in packs:
        gathered.append(gather_fronts(pack))
    assembled = None
    for picked in (slice(0, 1), slice(1, None)):
        steps = [block for blocks, _ in chunks[picked] for block in blocks]
        meta = jnp.concatenate([slot_meta, jnp.stack(steps).astype(jnp.int32)])
        counts = tuple(len(blocks) for blocks, _ in chunks[picked])
        assembled = place(meta, extend_map, gathered[picked], parent_base[0], row_dev, counts, assembled)
    return assembled[None]


def solution(mesh):
    placed = (
        P("front", "panel", None),
        P("front", "panel", None),
        P("front", None),
        P("front", "panel", None),
        P("front", "panel", None, None, None),
        P(),
        P(),
        P("front", "panel", None),
    )
    return jax.shard_map(body, mesh=mesh, in_specs=placed, out_specs=P("front", "panel", None), check_vma=False)
```

profile of v0, /device:TPU:10, one launch (start us, length us, event | category | flops | bytes accessed | tf_op | source)
XLA Modules:
  0.0 195.7 jit_solution(8837118237774846652)
XLA Ops:
  0.0 1.4 slice.9
  1.4 1.6 collective-permute-start.3
  3.0 1.3 slice.8
  4.3 0.6 collective-permute-start.1
  4.9 22.7 %collective-permute-done.3.refs_2_ = bf16[512,1024]{1,0:T(8,128)(2,1)} collective-permute-done((bf16[512,1024]{1,0:T(8,128)(2,1)S(1)}, bf16[512,1024]{1,0:T(8,128)(2,1)}, u32[]{:S(2)}, u32[]{:S(2)}) %collective-permute-start.3) | collective-permute-done | bytes 1048608 | tf_op jit(solution)/shard_map/ppermute | solution.py:43
  27.7 21.2 %collective-permute-done.1.refs_2_ = bf16[512,1024]{1,0:T(8,128)(2,1)S(1)} collective-permute-done((bf16[512,1024]{1,0:T(8,128)(2,1)S(1)}, bf16[512,1024]{1,0:T(8,128)(2,1)S(1)}, u32[]{:S(2)}, u32[]{:S(2)}) %collective-permute-start.1) | collective-permute-done | bytes 1048608 | tf_op jit(solution)/shard_map/ppermute | solution.py:43
  48.9 0.1 pad_add_fusion.meta
  49.0 1.6 copy-done.1
  50.6 5.5 %factor.3 = (bf16[512,1024]{1,0:T(8,128)(2,1)}, bf16[512,1024]{1,0:T(8,128)(2,1)S(1)}) custom-call(s32[4]{0:T(128)S(1)} %pad_add_fusion.meta, bf16[512,2048]{1,0:T(8,128)(2,1)S(1)} %bitcast.30, f32[1,2048]{1,0:T(1,128)S(1)} %copy-done.2, bf16[512,2048]{1,0:T(8,128)(2,1)S(1)} %bitcast.28, bf16[512,2048]{1,0:T(8,128)(2,1)} %collective-permute-done.refs_1_, ...), custom_call_target="tpu_custom_call" | custom-call | flops 2147483648 | bytes 4194304 | tf_op jit(solution)/shard_map/factor/pallas_call | solution.py:73
  56.1 0.5 collective-permute-start.7
  56.6 5.2 %factor.2 = (bf16[512,1024]{1,0:T(8,128)(2,1)}, bf16[512,1024]{1,0:T(8,128)(2,1)S(1)}) custom-call(s32[4]{0:T(128)S(1)} %pad_add_fusion.meta, bf16[512,2048]{1,0:T(8,128)(2,1)S(1)} %bitcast.31, f32[1,2048]{1,0:T(1,128)S(1)} %copy-done.2, bf16[512,2048]{1,0:T(8,128)(2,1)S(1)} %bitcast.29, bf16[512,2048]{1,0:T(8,128)(2,1)} %collective-permute-done.refs_1_, ...), custom_call_target="tpu_custom_call" | custom-call | flops 2147483648 | bytes 4194304 | tf_op jit(solution)/shard_map/factor/pallas_call | solution.py:73
  61.8 1.0 copy-done.4
  62.8 1.5 collective-permute-start.5
  64.3 0.1 collective-permute-start.26
  64.5 0.1 stack.83.meta
  64.5 1.4 broadcast_select_fusion
  66.0 0.6 collective-permute-start.17
  66.5 1.5 collective-permute-start.8
  68.1 21.0 %collective-permute-done.5.refs_4_.refs_6_ = bf16[512,1024]{1,0:T(8,128)(2,1)S(1)} collective-permute-done((bf16[512,1024]{1,0:T(8,128)(2,1)}, bf16[512,1024]{1,0:T(8,128)(2,1)S(1)}, u32[]{:S(2)}, u32[]{:S(2)}) %collective-permute-start.5) | collective-permute-done | bytes 1048608 | tf_op jit(solution)/shard_map/ppermute | solution.py:43
  89.1 11.7 %compress.5.refs_0_ = bf16[2,2,4,32,256]{4,3,2,1,0:T(8,128)(2,1)S(1)} custom-call(s32[8]{0:T(128)S(1)} %stack.83.meta, bf16[512,1024]{1,0:T(8,128)(2,1)} %copy-done.4, bf16[512,1024]{1,0:T(8,128)(2,1)} %copy-done.3, f32[512,2048]{1,0:T(8,128)} %bitcast.34, f32[2,8,32,256]{3,2,1,0:T(8,128)} %bitcast.37, bf16[512,1024]{1,0:T(8,128)(2,1)} %get-tuple-element.11.refs_4_, ...), custom_call_target="tpu_custom_call" | custom-call | flops 8589934592 | bytes 8388608 | tf_op jit(solution)/shard_map/compress/pallas_call | solution.py:210
  100.8 2.7 %collective-permute-start.30 = (bf16[2,2,4,32,256]{4,3,2,1,0:T(8,128)(2,1)S(1)}, bf16[2,2,4,32,256]{4,3,2,1,0:T(8,128)(2,1)}, u32[]{:S(2)}, u32[]{:S(2)}) collective-permute-start(bf16[2,2,4,32,256]{4,3,2,1,0:T(8,128)(2,1)S(1)} %compress.5.refs_0_), channel_id=1, source_target_pairs={{0,16},{4,20},{8,24},{12,28},{16,0},{20,4},{24,8},{28,12},{1,17},{... | collective-permute-start | bytes 786440 | tf_op jit(solution)/shard_map/ppermute | solution.py:43
  103.5 7.6 %collective-permute-done.8.refs_8_ = bf16[256,1024]{1,0:T(8,128)(2,1)} collective-permute-done((bf16[256,1024]{1,0:T(8,128)(2,1)S(1)}, bf16[256,1024]{1,0:T(8,128)(2,1)}, u32[]{:S(2)}, u32[]{:S(2)}) %collective-permute-start.8) | collective-permute-done | bytes 524320 | tf_op jit(solution)/shard_map/ppermute | solution.py:43
  111.1 0.5 collective-permute-start.28
  111.5 3.8 %collective-permute-done.30.refs_4_ = bf16[2,2,4,32,256]{4,3,2,1,0:T(8,128)(2,1)} collective-permute-done((bf16[2,2,4,32,256]{4,3,2,1,0:T(8,128)(2,1)S(1)}, bf16[2,2,4,32,256]{4,3,2,1,0:T(8,128)(2,1)}, u32[]{:S(2)}, u32[]{:S(2)}) %collective-permute-start.30) | collective-permute-done | bytes 262176 | tf_op jit(solution)/shard_map/ppermute | solution.py:43
  115.3 1.5 collective-permute-start.32
  116.8 0.2 reduce-window.8
  117.0 0.1 stack.72.meta
  117.1 0.1 stack.80.meta
  117.2 0.1 collective-permute-start.18
  117.3 3.1 %collective-permute-done.28.refs_2_ = bf16[2,2,4,32,256]{4,3,2,1,0:T(8,128)(2,1)} collective-permute-done((bf16[2,2,4,32,256]{4,3,2,1,0:T(8,128)(2,1)S(1)}, bf16[2,2,4,32,256]{4,3,2,1,0:T(8,128)(2,1)}, u32[]{:S(2)}, u32[]{:S(2)}) %collective-permute-start.28) | collective-permute-done | bytes 262176 | tf_op jit(solution)/shard_map/ppermute | solution.py:43
  120.3 0.5 collective-permute-start.27
  120.9 4.6 %collective-permute-done.32.refs_6_ = bf16[2,2,4,32,256]{4,3,2,1,0:T(8,128)(2,1)} collective-permute-done((bf16[2,2,4,32,256]{4,3,2,1,0:T(8,128)(2,1)}, bf16[2,2,4,32,256]{4,3,2,1,0:T(8,128)(2,1)}, u32[]{:S(2)}, u32[]{:S(2)}) %collective-permute-start.32) | collective-permute-done | bytes 262176 | tf_op jit(solution)/shard_map/ppermute | solution.py:43
  125.5 0.5 collective-permute-start.31
  126.0 1.5 collective-permute-start.29
  127.5 0.5 collective-permute-start.33
  128.1 0.4 copy-done.11
  128.5 9.9 %compress.3.refs_0_ = bf16[2,2,2,32,256]{4,3,2,1,0:T(8,128)(2,1)S(1)} custom-call(s32[8]{0:T(128)S(1)} %stack.72.meta, bf16[512,1024]{1,0:T(8,128)(2,1)} %copy-done.4, bf16[512,1024]{1,0:T(8,128)(2,1)} %copy-done.3, f32[512,2048]{1,0:T(8,128)} %bitcast.35, f32[2,8,32,256]{3,2,1,0:T(8,128)} %bitcast.38, bf16[512,1024]{1,0:T(8,128)(2,1)} %copy-done.10, ...), custom_call_target="tpu_custom_call" | custom-call | flops 4294967296 | bytes 8388608 | tf_op jit(solution)/shard_map/compress/pallas_call | solution.py:210
  138.4 4.5 %collective-permute-start.13 = (bf16[2,2,2,32,256]{4,3,2,1,0:T(8,128)(2,1)S(1)}, bf16[2,2,2,32,256]{4,3,2,1,0:T(8,128)(2,1)S(1)}, u32[]{:S(2)}, u32[]{:S(2)}) collective-permute-start(bf16[2,2,2,32,256]{4,3,2,1,0:T(8,128)(2,1)S(1)} %compress.3.refs_0_), channel_id=1, source_target_pairs={{0,16},{4,20},{8,24},{12,28},{16,0},{20,4},{24,8},{28,12},{1,17},{... | collective-permute-start | bytes 393224 | tf_op jit(solution)/shard_map/ppermute | solution.py:43
  142.9 9.7 %compress.4.refs_8_ = bf16[2,2,2,32,256]{4,3,2,1,0:T(8,128)(2,1)S(1)} custom-call(s32[8]{0:T(128)S(1)} %stack.80.meta, bf16[512,1024]{1,0:T(8,128)(2,1)} %copy-done.4, bf16[512,1024]{1,0:T(8,128)(2,1)} %copy-done.3, f32[512,2048]{1,0:T(8,128)} %bitcast.36, f32[2,8,32,256]{3,2,1,0:T(8,128)} %bitcast.39, bf16[512,1024]{1,0:T(8,128)(2,1)} %copy-done.10, ...), custom_call_target="tpu_custom_call" | custom-call | flops 4294967296 | bytes 8388608 | tf_op jit(solution)/shard_map/compress/pallas_call | solution.py:210
  152.7 0.1 collective-permute-start.11
  152.8 1.1 collective-permute-start.10
  153.9 0.9 collective-permute-start.22
  154.8 0.1 select_reduce_fusion
  154.9 1.9 collective-permute-start.20
  156.8 1.0 collective-permute-start.19
  157.8 1.3 collective-permute-done.11.refs_2_
  159.1 1.1 collective-permute-start.14
  160.2 0.9 collective-permute-done.22.refs_12_
  161.2 2.1 %collective-permute-start.24 = (bf16[2,2,2,32,256]{4,3,2,1,0:T(8,128)(2,1)S(1)}, bf16[2,2,2,32,256]{4,3,2,1,0:T(8,128)(2,1)S(1)}, u32[]{:S(2)}, u32[]{:S(2)}) collective-permute-start(bf16[2,2,2,32,256]{4,3,2,1,0:T(8,128)(2,1)S(1)} %collective-permute-done.22.refs_12_), channel_id=1, source_target_pairs={{0,8},{4,12},{8,0},{12,4},{16,24},{20,28},{24,16},{28,20},{1,9},{5... | collective-permute-start | bytes 393224 | tf_op jit(solution)/shard_map/ppermute | solution.py:43
  163.3 0.1 concatenate.10.meta
  163.4 0.1 concatenate.9.meta
  163.5 1.2 collective-permute-done.20.refs_10_
  164.7 1.1 collective-permute-start.23
  165.8 1.0 collective-permute-start.12
  166.7 0.4 collective-permute-done.15.refs_6_
  167.2 1.1 collective-permute-start.21
  168.3 0.9 collective-permute-start.16
  169.2 1.1 collective-permute-start.25
  170.4 11.8 %place.2.refs_16_ = bf16[1024,4096]{1,0:T(8,128)(2,1)} custom-call(s32[11]{0:T(128)S(1)} %concatenate.10.meta, s32[8,2048]{1,0:T(8,128)S(1)} %copy-done.8, bf16[1024,4096]{1,0:T(8,128)(2,1)} %bitcast.32, bf16[2,2,4,32,256]{4,3,2,1,0:T(8,128)(2,1)} %copy-done.5, bf16[2,2,4,32,256]{4,3,2,1,0:T(8,128)(2,1)} %copy-done.14, ...), custom_call_target="tpu_custom_call" | custom-call | flops 8589934592 | bytes 8388608 | tf_op jit(solution)/shard_map/place/pallas_call | solution.py:330
  182.4 0.6 copy-done.28
  183.0 0.1 copy-done.27
  183.0 0.1 copy-done.29
  183.1 0.6 copy-done.31
  183.8 11.8 %place.3 = bf16[1024,4096]{1,0:T(8,128)(2,1)} custom-call(s32[11]{0:T(128)S(1)} %concatenate.9.meta, s32[8,2048]{1,0:T(8,128)S(1)} %copy-done.8, bf16[1024,4096]{1,0:T(8,128)(2,1)} %bitcast.33, bf16[2,2,2,32,256]{4,3,2,1,0:T(8,128)(2,1)} %copy-done.6, bf16[2,2,2,32,256]{4,3,2,1,0:T(8,128)(2,1)} %copy-done.20, ...), custom_call_target="tpu_custom_call", output_to_operand_aliasing={{}: (19, {})} | custom-call | flops 8589934592 | bytes 8388608 | tf_op jit(solution)/shard_map/place/pallas_call | solution.py:330
  (91 shorter events, 0.2 us)
Async XLA Ops:
  0.0 49.0 %copy-start = (bf16[1,512,2048]{2,1,0:T(8,128)(2,1)S(1)}, bf16[1,512,2048]{2,1,0:T(8,128)(2,1)}, u32[]{:S(2)}) copy-start(bf16[1,512,2048]{2,1,0:T(8,128)(2,1)} %param.9) | copy-start | bytes 6291460
  0.0 49.0 %copy-start.2 = (f32[1,2048]{1,0:T(1,128)S(1)}, f32[1,2048]{1,0:T(1,128)}, u32[]{:S(2)}) copy-start(f32[1,2048]{1,0:T(1,128)} %pivots.3) | copy-start | bytes 24580
  1.4 26.2 %collective-permute-start.3 = (bf16[512,1024]{1,0:T(8,128)(2,1)S(1)}, bf16[512,1024]{1,0:T(8,128)(2,1)}, u32[]{:S(2)}, u32[]{:S(2)}) collective-permute-start(bf16[512,1024]{1,0:T(8,128)(2,1)S(1)} %slice.9), channel_id=1, source_target_pairs={{0,2},{1,3},{2,0},{3,1},{4,6},{5,7},{6,4},{7,5},{8,10},{9,11},{10,... | collective-permute-start | bytes 3145736 | tf_op jit(solution)/shard_map/ppermute | solution.py:43
  3.0 45.9 %collective-permute-start = (bf16[512,2048]{1,0:T(8,128)(2,1)}, bf16[512,2048]{1,0:T(8,128)(2,1)}, u32[]{:S(2)}, u32[]{:S(2)}) collective-permute-start(bf16[512,2048]{1,0:T(8,128)(2,1)} %bitcast.26), channel_id=1, source_target_pairs={{0,1},{1,0},{2,3},{3,2},{4,5},{5,4},{6,7},{7,6},{8,9},{9,8},{10,11... | collective-permute-start | bytes 6291464 | tf_op jit(solution)/shard_map/ppermute | solution.py:43
  4.3 44.5 %collective-permute-start.1 = (bf16[512,1024]{1,0:T(8,128)(2,1)S(1)}, bf16[512,1024]{1,0:T(8,128)(2,1)S(1)}, u32[]{:S(2)}, u32[]{:S(2)}) collective-permute-start(bf16[512,1024]{1,0:T(8,128)(2,1)S(1)} %slice.8), channel_id=1, source_target_pairs={{0,2},{1,3},{2,0},{3,1},{4,6},{5,7},{6,4},{7,5},{8,10},{9,11},{10,... | collective-permute-start | bytes 3145736 | tf_op jit(solution)/shard_map/ppermute | solution.py:43
  27.6 21.3 %collective-permute-start.4 = (bf16[512,1024]{1,0:T(8,128)(2,1)}, bf16[512,1024]{1,0:T(8,128)(2,1)}, u32[]{:S(2)}, u32[]{:S(2)}) collective-permute-start(bf16[512,1024]{1,0:T(8,128)(2,1)} %collective-permute-done.3.refs_2_), channel_id=1, source_target_pairs={{0,1},{1,0},{2,3},{3,2},{4,5},{5,4},{6,7},{7,6},{8,9},{9,8},{10,11... | collective-permute-start | bytes 3145736 | tf_op jit(solution)/shard_map/ppermute | solution.py:43
  48.9 7.7 %collective-permute-start.2 = (bf16[512,1024]{1,0:T(8,128)(2,1)S(1)}, bf16[512,1024]{1,0:T(8,128)(2,1)}, u32[]{:S(2)}, u32[]{:S(2)}) collective-permute-start(bf16[512,1024]{1,0:T(8,128)(2,1)S(1)} %collective-permute-done.1.refs_2_), channel_id=1, source_target_pairs={{0,1},{1,0},{2,3},{3,2},{4,5},{5,4},{6,7},{7,6},{8,9},{9,8},{10,11... | collective-permute-start | bytes 3145736 | tf_op jit(solution)/shard_map/ppermute | solution.py:43
  49.0 1.6 copy-start.1
  56.1 5.7 %copy-start.3 = (bf16[512,1024]{1,0:T(8,128)(2,1)}, bf16[512,1024]{1,0:T(8,128)(2,1)S(1)}, u32[]{:S(2)}) copy-start(bf16[512,1024]{1,0:T(8,128)(2,1)S(1)} %get-tuple-element.10.refs_1_) | copy-start | bytes 3145732
  56.1 8.5 %collective-permute-start.7 = (bf16[512,1024]{1,0:T(8,128)(2,1)}, bf16[512,1024]{1,0:T(8,128)(2,1)}, u32[]{:S(2)}, u32[]{:S(2)}) collective-permute-start(bf16[512,1024]{1,0:T(8,128)(2,1)} %get-tuple-element.12.refs_6_), channel_id=1, source_target_pairs={{0,1},{1,0},{2,3},{3,2},{4,5},{5,4},{6,7},{7,6},{8,9},{9,8},{10,11... | collective-permute-start | bytes 3145736 | tf_op jit(solution)/shard_map/ppermute | solution.py:43
  61.8 1.0 copy-start.4
  62.8 26.2 %collective-permute-start.5 = (bf16[512,1024]{1,0:T(8,128)(2,1)}, bf16[512,1024]{1,0:T(8,128)(2,1)S(1)}, u32[]{:S(2)}, u32[]{:S(2)}) collective-permute-start(bf16[512,1024]{1,0:T(8,128)(2,1)} %get-tuple-element.11.refs_4_), channel_id=1, source_target_pairs={{0,2},{1,3},{2,0},{3,1},{4,6},{5,7},{6,4},{7,5},{8,10},{9,11},{10,... | collective-permute-start | bytes 3145736 | tf_op jit(solution)/shard_map/ppermute | solution.py:43
  64.3 24.7 %collective-permute-start.26 = (bf16[512,1024]{1,0:T(8,128)(2,1)}, bf16[512,1024]{1,0:T(8,128)(2,1)}, u32[]{:S(2)}, u32[]{:S(2)}) collective-permute-start(bf16[512,1024]{1,0:T(8,128)(2,1)} %get-tuple-element.11.refs_4_), channel_id=1, source_target_pairs={{0,1},{1,0},{2,3},{3,2},{4,5},{5,4},{6,7},{7,6},{8,9},{9,8},{10,11... | collective-permute-start | bytes 3145736 | tf_op jit(solution)/shard_map/ppermute | solution.py:43
  66.0 51.2 %collective-permute-start.17 = (bf16[256,1024]{1,0:T(8,128)(2,1)S(1)}, bf16[256,1024]{1,0:T(8,128)(2,1)S(1)}, u32[]{:S(2)}, u32[]{:S(2)}) collective-permute-start(bf16[256,1024]{1,0:T(8,128)(2,1)S(1)} %get-tuple-element.15), channel_id=1, source_target_pairs={{0,2},{1,3},{2,0},{3,1},{4,6},{5,7},{6,4},{7,5},{8,10},{9,11},{10,... | collective-permute-start | bytes 1572872 | tf_op jit(solution)/shard_map/ppermute | solution.py:43
  66.5 44.5 %collective-permute-start.8 = (bf16[256,1024]{1,0:T(8,128)(2,1)S(1)}, bf16[256,1024]{1,0:T(8,128)(2,1)}, u32[]{:S(2)}, u32[]{:S(2)}) collective-permute-start(bf16[256,1024]{1,0:T(8,128)(2,1)S(1)} %get-tuple-element.16), channel_id=1, source_target_pairs={{0,2},{1,3},{2,0},{3,1},{4,6},{5,7},{6,4},{7,5},{8,10},{9,11},{10,... | collective-permute-start | bytes 1572872 | tf_op jit(solution)/shard_map/ppermute | solution.py:43
  89.1 11.8 %copy-start.10 = (bf16[512,1024]{1,0:T(8,128)(2,1)}, bf16[512,1024]{1,0:T(8,128)(2,1)S(1)}, u32[]{:S(2)}) copy-start(bf16[512,1024]{1,0:T(8,128)(2,1)S(1)} %collective-permute-done.5.refs_4_.refs_6_) | copy-start | bytes 3145732
  89.1 38.5 %collective-permute-start.6 = (bf16[512,1024]{1,0:T(8,128)(2,1)S(1)}, bf16[512,1024]{1,0:T(8,128)(2,1)S(1)}, u32[]{:S(2)}, u32[]{:S(2)}) collective-permute-start(bf16[512,1024]{1,0:T(8,128)(2,1)S(1)} %collective-permute-done.5.refs_4_.refs_6_), channel_id=1, source_target_pairs={{0,1},{1,0},{2,3},{3,2},{4,5},{5,4},{6,7},{7,6},{8,9},{9,8},{10,11... | collective-permute-start | bytes 3145736 | tf_op jit(solution)/shard_map/ppermute | solution.py:43
  89.1 27.7 %copy-start.9 = (s32[8]{0:T(128)S(1)}, s32[8]{0:T(128)}, u32[]{:S(2)}) copy-start(s32[8]{0:T(128)} %param.14) | copy-start | bytes 100
  100.8 37.5 %copy-start.5 = (bf16[2,2,4,32,256]{4,3,2,1,0:T(8,128)(2,1)}, bf16[2,2,4,32,256]{4,3,2,1,0:T(8,128)(2,1)S(1)}, u32[]{:S(2)}) copy-start(bf16[2,2,4,32,256]{4,3,2,1,0:T(8,128)(2,1)S(1)} %compress.5.refs_0_) | copy-start | bytes 786436
  100.8 14.4 %collective-permute-start.30 = (bf16[2,2,4,32,256]{4,3,2,1,0:T(8,128)(2,1)S(1)}, bf16[2,2,4,32,256]{4,3,2,1,0:T(8,128)(2,1)}, u32[]{:S(2)}, u32[]{:S(2)}) collective-permute-start(bf16[2,2,4,32,256]{4,3,2,1,0:T(8,128)(2,1)S(1)} %compress.5.refs_0_), channel_id=1, source_target_pairs={{0,16},{4,20},{8,24},{12,28},{16,0},{20,4},{24,8},{28,12},{1,17},{... | collective-permute-start | bytes 786440 | tf_op jit(solution)/shard_map/ppermute | solution.py:43
  111.1 15.0 %collective-permute-start.9 = (bf16[256,1024]{1,0:T(8,128)(2,1)}, bf16[256,1024]{1,0:T(8,128)(2,1)}, u32[]{:S(2)}, u32[]{:S(2)}) collective-permute-start(bf16[256,1024]{1,0:T(8,128)(2,1)} %collective-permute-done.8.refs_8_), channel_id=1, source_target_pairs={{0,1},{1,0},{2,3},{3,2},{4,5},{5,4},{6,7},{7,6},{8,9},{9,8},{10,11... | collective-permute-start | bytes 1572872 | tf_op jit(solution)/shard_map/ppermute | solution.py:43
  111.1 9.3 %collective-permute-start.28 = (bf16[2,2,4,32,256]{4,3,2,1,0:T(8,128)(2,1)S(1)}, bf16[2,2,4,32,256]{4,3,2,1,0:T(8,128)(2,1)}, u32[]{:S(2)}, u32[]{:S(2)}) collective-permute-start(bf16[2,2,4,32,256]{4,3,2,1,0:T(8,128)(2,1)S(1)} %compress.5.refs_0_), channel_id=1, source_target_pairs={{0,8},{4,12},{8,0},{12,4},{16,24},{20,28},{24,16},{28,20},{1,9},{5... | collective-permute-start | bytes 786440 | tf_op jit(solution)/shard_map/ppermute | solution.py:43
  115.3 10.2 %collective-permute-start.32 = (bf16[2,2,4,32,256]{4,3,2,1,0:T(8,128)(2,1)}, bf16[2,2,4,32,256]{4,3,2,1,0:T(8,128)(2,1)}, u32[]{:S(2)}, u32[]{:S(2)}) collective-permute-start(bf16[2,2,4,32,256]{4,3,2,1,0:T(8,128)(2,1)} %collective-permute-done.30.refs_4_), channel_id=1, source_target_pairs={{0,8},{4,12},{8,0},{12,4},{16,24},{20,28},{24,16},{28,20},{1,9},{5... | collective-permute-start | bytes 786440 | tf_op jit(solution)/shard_map/ppermute | solution.py:43
  117.2 25.8 %copy-start.12 = (bf16[256,1024]{1,0:T(8,128)(2,1)}, bf16[256,1024]{1,0:T(8,128)(2,1)S(1)}, u32[]{:S(2)}) copy-start(bf16[256,1024]{1,0:T(8,128)(2,1)S(1)} %collective-permute-done.17.refs_8_) | copy-start | bytes 1572868
  117.2 21.2 %collective-permute-start.18 = (bf16[256,1024]{1,0:T(8,128)(2,1)S(1)}, bf16[256,1024]{1,0:T(8,128)(2,1)S(1)}, u32[]{:S(2)}, u32[]{:S(2)}) collective-permute-start(bf16[256,1024]{1,0:T(8,128)(2,1)S(1)} %collective-permute-done.17.refs_8_), channel_id=1, source_target_pairs={{0,1},{1,0},{2,3},{3,2},{4,5},{5,4},{6,7},{7,6},{8,9},{9,8},{10,11... | collective-permute-start | bytes 1572872 | tf_op jit(solution)/shard_map/ppermute | solution.py:43
  120.3 32.3 %collective-permute-start.27 = (bf16[2,2,4,32,256]{4,3,2,1,0:T(8,128)(2,1)S(1)}, bf16[2,2,4,32,256]{4,3,2,1,0:T(8,128)(2,1)S(1)}, u32[]{:S(2)}, u32[]{:S(2)}) collective-permute-start(bf16[2,2,4,32,256]{4,3,2,1,0:T(8,128)(2,1)S(1)} %compress.5.refs_0_), channel_id=1, source_target_pairs={{0,4},{4,0},{8,12},{12,8},{16,20},{20,16},{24,28},{28,24},{1,5},{5... | collective-permute-start | bytes 786440 | tf_op jit(solution)/shard_map/ppermute | solution.py:43
  125.5 27.2 %collective-permute-start.31 = (bf16[2,2,4,32,256]{4,3,2,1,0:T(8,128)(2,1)}, bf16[2,2,4,32,256]{4,3,2,1,0:T(8,128)(2,1)S(1)}, u32[]{:S(2)}, u32[]{:S(2)}) collective-permute-start(bf16[2,2,4,32,256]{4,3,2,1,0:T(8,128)(2,1)} %collective-permute-done.30.refs_4_), channel_id=1, source_target_pairs={{0,4},{4,0},{8,12},{12,8},{16,20},{20,16},{24,28},{28,24},{1,5},{5... | collective-permute-start | bytes 786440 | tf_op jit(solution)/shard_map/ppermute | solution.py:43
  126.0 27.9 %collective-permute-start.29 = (bf16[2,2,4,32,256]{4,3,2,1,0:T(8,128)(2,1)}, bf16[2,2,4,32,256]{4,3,2,1,0:T(8,128)(2,1)S(1)}, u32[]{:S(2)}, u32[]{:S(2)}) collective-permute-start(bf16[2,2,4,32,256]{4,3,2,1,0:T(8,128)(2,1)} %collective-permute-done.28.refs_2_), channel_id=1, source_target_pairs={{0,4},{4,0},{8,12},{12,8},{16,20},{20,16},{24,28},{28,24},{1,5},{5... | collective-permute-start | bytes 786440 | tf_op jit(solution)/shard_map/ppermute | solution.py:43
  127.5 1.0 copy-start.11
  127.5 27.4 %collective-permute-start.33 = (bf16[2,2,4,32,256]{4,3,2,1,0:T(8,128)(2,1)}, bf16[2,2,4,32,256]{4,3,2,1,0:T(8,128)(2,1)S(1)}, u32[]{:S(2)}, u32[]{:S(2)}) collective-permute-start(bf16[2,2,4,32,256]{4,3,2,1,0:T(8,128)(2,1)} %collective-permute-done.32.refs_6_), channel_id=1, source_target_pairs={{0,4},{4,0},{8,12},{12,8},{16,20},{20,16},{24,28},{28,24},{1,5},{5... | collective-permute-start | bytes 786440 | tf_op jit(solution)/shard_map/ppermute | solution.py:43
  138.4 14.4 %copy-start.6 = (bf16[2,2,2,32,256]{4,3,2,1,0:T(8,128)(2,1)}, bf16[2,2,2,32,256]{4,3,2,1,0:T(8,128)(2,1)S(1)}, u32[]{:S(2)}) copy-start(bf16[2,2,2,32,256]{4,3,2,1,0:T(8,128)(2,1)S(1)} %compress.3.refs_0_) | copy-start | bytes 393220
  138.4 32.0 %copy-start.8 = (s32[8,2048]{1,0:T(8,128)S(1)}, s32[8,2048]{1,0:T(8,128)}, u32[]{:S(2)}) copy-start(s32[8,2048]{1,0:T(8,128)} %maps.3) | copy-start | bytes 196612
  138.4 4.5 %copy-start.13 = (bf16[256,1024]{1,0:T(8,128)(2,1)}, bf16[256,1024]{1,0:T(8,128)(2,1)S(1)}, u32[]{:S(2)}) copy-start(bf16[256,1024]{1,0:T(8,128)(2,1)S(1)} %collective-permute-done.18.refs_9_) | copy-start | bytes 1572868
  138.4 18.4 %collective-permute-start.13 = (bf16[2,2,2,32,256]{4,3,2,1,0:T(8,128)(2,1)S(1)}, bf16[2,2,2,32,256]{4,3,2,1,0:T(8,128)(2,1)S(1)}, u32[]{:S(2)}, u32[]{:S(2)}) collective-permute-start(bf16[2,2,2,32,256]{4,3,2,1,0:T(8,128)(2,1)S(1)} %compress.3.refs_0_), channel_id=1, source_target_pairs={{0,16},{4,20},{8,24},{12,28},{16,0},{20,4},{24,8},{28,12},{1,17},{... | collective-permute-start | bytes 393224 | tf_op jit(solution)/shard_map/ppermute | solution.py:43
  152.6 29.6 %copy-start.7 = (bf16[2,2,2,32,256]{4,3,2,1,0:T(8,128)(2,1)}, bf16[2,2,2,32,256]{4,3,2,1,0:T(8,128)(2,1)S(1)}, u32[]{:S(2)}) copy-start(bf16[2,2,2,32,256]{4,3,2,1,0:T(8,128)(2,1)S(1)} %compress.4.refs_8_) | copy-start | bytes 393220
  152.7 10.6 %copy-start.14 = (bf16[2,2,4,32,256]{4,3,2,1,0:T(8,128)(2,1)}, bf16[2,2,4,32,256]{4,3,2,1,0:T(8,128)(2,1)S(1)}, u32[]{:S(2)}) copy-start(bf16[2,2,4,32,256]{4,3,2,1,0:T(8,128)(2,1)S(1)} %collective-permute-done.27.refs_1_) | copy-start | bytes 786436
  152.7 6.4 %collective-permute-start.11 = (bf16[2,2,2,32,256]{4,3,2,1,0:T(8,128)(2,1)S(1)}, bf16[2,2,2,32,256]{4,3,2,1,0:T(8,128)(2,1)S(1)}, u32[]{:S(2)}, u32[]{:S(2)}) collective-permute-start(bf16[2,2,2,32,256]{4,3,2,1,0:T(8,128)(2,1)S(1)} %compress.3.refs_0_), channel_id=1, source_target_pairs={{0,8},{4,12},{8,0},{12,4},{16,24},{20,28},{24,16},{28,20},{1,9},{5... | collective-permute-start | bytes 393224 | tf_op jit(solution)/shard_map/ppermute | solution.py:43
  152.8 10.5 %copy-start.15 = (bf16[2,2,4,32,256]{4,3,2,1,0:T(8,128)(2,1)}, bf16[2,2,4,32,256]{4,3,2,1,0:T(8,128)(2,1)S(1)}, u32[]{:S(2)}) copy-start(bf16[2,2,4,32,256]{4,3,2,1,0:T(8,128)(2,1)S(1)} %collective-permute-done.31.refs_5_) | copy-start | bytes 786436
  152.8 6.3 %collective-permute-start.10 = (bf16[2,2,2,32,256]{4,3,2,1,0:T(8,128)(2,1)S(1)}, bf16[2,2,2,32,256]{4,3,2,1,0:T(8,128)(2,1)S(1)}, u32[]{:S(2)}, u32[]{:S(2)}) collective-permute-start(bf16[2,2,2,32,256]{4,3,2,1,0:T(8,128)(2,1)S(1)} %compress.3.refs_0_), channel_id=1, source_target_pairs={{0,4},{4,0},{8,12},{12,8},{16,20},{20,16},{24,28},{28,24},{1,5},{5... | collective-permute-start | bytes 393224 | tf_op jit(solution)/shard_map/ppermute | solution.py:43
  153.9 9.4 %copy-start.16 = (bf16[2,2,4,32,256]{4,3,2,1,0:T(8,128)(2,1)}, bf16[2,2,4,32,256]{4,3,2,1,0:T(8,128)(2,1)S(1)}, u32[]{:S(2)}) copy-start(bf16[2,2,4,32,256]{4,3,2,1,0:T(8,128)(2,1)S(1)} %collective-permute-done.29.refs_3_) | copy-start | bytes 786436
  153.9 7.3 %collective-permute-start.22 = (bf16[2,2,2,32,256]{4,3,2,1,0:T(8,128)(2,1)S(1)}, bf16[2,2,2,32,256]{4,3,2,1,0:T(8,128)(2,1)S(1)}, u32[]{:S(2)}, u32[]{:S(2)}) collective-permute-start(bf16[2,2,2,32,256]{4,3,2,1,0:T(8,128)(2,1)S(1)} %compress.4.refs_8_), channel_id=1, source_target_pairs={{0,16},{4,20},{8,24},{12,28},{16,0},{20,4},{24,8},{28,12},{1,17},{... | collective-permute-start | bytes 393224 | tf_op jit(solution)/shard_map/ppermute | solution.py:43
  154.9 15.5 %copy-start.17 = (bf16[2,2,4,32,256]{4,3,2,1,0:T(8,128)(2,1)}, bf16[2,2,4,32,256]{4,3,2,1,0:T(8,128)(2,1)S(1)}, u32[]{:S(2)}) copy-start(bf16[2,2,4,32,256]{4,3,2,1,0:T(8,128)(2,1)S(1)} %collective-permute-done.33.refs_7_) | copy-start | bytes 786436
  154.9 9.8 %collective-permute-start.20 = (bf16[2,2,2,32,256]{4,3,2,1,0:T(8,128)(2,1)S(1)}, bf16[2,2,2,32,256]{4,3,2,1,0:T(8,128)(2,1)S(1)}, u32[]{:S(2)}, u32[]{:S(2)}) collective-permute-start(bf16[2,2,2,32,256]{4,3,2,1,0:T(8,128)(2,1)S(1)} %compress.4.refs_8_), channel_id=1, source_target_pairs={{0,8},{4,12},{8,0},{12,4},{16,24},{20,28},{24,16},{28,20},{1,9},{5... | collective-permute-start | bytes 393224 | tf_op jit(solution)/shard_map/ppermute | solution.py:43
  156.8 25.4 %copy-start.18 = (bf16[2,2,2,32,256]{4,3,2,1,0:T(8,128)(2,1)}, bf16[2,2,2,32,256]{4,3,2,1,0:T(8,128)(2,1)S(1)}, u32[]{:S(2)}) copy-start(bf16[2,2,2,32,256]{4,3,2,1,0:T(8,128)(2,1)S(1)} %collective-permute-done.13.refs_4_) | copy-start | bytes 393220
  156.8 9.0 %collective-permute-start.19 = (bf16[2,2,2,32,256]{4,3,2,1,0:T(8,128)(2,1)S(1)}, bf16[2,2,2,32,256]{4,3,2,1,0:T(8,128)(2,1)S(1)}, u32[]{:S(2)}, u32[]{:S(2)}) collective-permute-start(bf16[2,2,2,32,256]{4,3,2,1,0:T(8,128)(2,1)S(1)} %compress.4.refs_8_), channel_id=1, source_target_pairs={{0,4},{4,0},{8,12},{12,8},{16,20},{20,16},{24,28},{28,24},{1,5},{5... | collective-permute-start | bytes 393224 | tf_op jit(solution)/shard_map/ppermute | solution.py:43
  159.1 23.1 %copy-start.19 = (bf16[2,2,2,32,256]{4,3,2,1,0:T(8,128)(2,1)}, bf16[2,2,2,32,256]{4,3,2,1,0:T(8,128)(2,1)S(1)}, u32[]{:S(2)}) copy-start(bf16[2,2,2,32,256]{4,3,2,1,0:T(8,128)(2,1)S(1)} %collective-permute-done.11.refs_2_) | copy-start | bytes 393220
  159.1 8.1 %collective-permute-start.15 = (bf16[2,2,2,32,256]{4,3,2,1,0:T(8,128)(2,1)S(1)}, bf16[2,2,2,32,256]{4,3,2,1,0:T(8,128)(2,1)S(1)}, u32[]{:S(2)}, u32[]{:S(2)}) collective-permute-start(bf16[2,2,2,32,256]{4,3,2,1,0:T(8,128)(2,1)S(1)} %collective-permute-done.13.refs_4_), channel_id=1, source_target_pairs={{0,8},{4,12},{8,0},{12,4},{16,24},{20,28},{24,16},{28,20},{1,9},{5... | collective-permute-start | bytes 393224 | tf_op jit(solution)/shard_map/ppermute | solution.py:43
  159.1 23.1 %copy-start.20 = (bf16[2,2,2,32,256]{4,3,2,1,0:T(8,128)(2,1)}, bf16[2,2,2,32,256]{4,3,2,1,0:T(8,128)(2,1)S(1)}, u32[]{:S(2)}) copy-start(bf16[2,2,2,32,256]{4,3,2,1,0:T(8,128)(2,1)S(1)} %collective-permute-done.10.refs_1_) | copy-start | bytes 393220
  159.1 9.2 %collective-permute-start.14 = (bf16[2,2,2,32,256]{4,3,2,1,0:T(8,128)(2,1)S(1)}, bf16[2,2,2,32,256]{4,3,2,1,0:T(8,128)(2,1)S(1)}, u32[]{:S(2)}, u32[]{:S(2)}) collective-permute-start(bf16[2,2,2,32,256]{4,3,2,1,0:T(8,128)(2,1)S(1)} %collective-permute-done.13.refs_4_), channel_id=1, source_target_pairs={{0,4},{4,0},{8,12},{12,8},{16,20},{20,16},{24,28},{28,24},{1,5},{5... | collective-permute-start | bytes 393224 | tf_op jit(solution)/shard_map/ppermute | solution.py:43
  161.2 21.1 %copy-start.21 = (bf16[2,2,2,32,256]{4,3,2,1,0:T(8,128)(2,1)}, bf16[2,2,2,32,256]{4,3,2,1,0:T(8,128)(2,1)S(1)}, u32[]{:S(2)}) copy-start(bf16[2,2,2,32,256]{4,3,2,1,0:T(8,128)(2,1)S(1)} %collective-permute-done.22.refs_12_) | copy-start | bytes 393220
  161.2 8.1 %collective-permute-start.24 = (bf16[2,2,2,32,256]{4,3,2,1,0:T(8,128)(2,1)S(1)}, bf16[2,2,2,32,256]{4,3,2,1,0:T(8,128)(2,1)S(1)}, u32[]{:S(2)}, u32[]{:S(2)}) collective-permute-start(bf16[2,2,2,32,256]{4,3,2,1,0:T(8,128)(2,1)S(1)} %collective-permute-done.22.refs_12_), channel_id=1, source_target_pairs={{0,8},{4,12},{8,0},{12,4},{16,24},{20,28},{24,16},{28,20},{1,9},{5... | collective-permute-start | bytes 393224 | tf_op jit(solution)/shard_map/ppermute | solution.py:43
  164.7 17.6 %copy-start.22 = (bf16[2,2,2,32,256]{4,3,2,1,0:T(8,128)(2,1)}, bf16[2,2,2,32,256]{4,3,2,1,0:T(8,128)(2,1)S(1)}, u32[]{:S(2)}) copy-start(bf16[2,2,2,32,256]{4,3,2,1,0:T(8,128)(2,1)S(1)} %collective-permute-done.20.refs_10_) | copy-start | bytes 393220
  164.7 17.6 %collective-permute-start.23 = (bf16[2,2,2,32,256]{4,3,2,1,0:T(8,128)(2,1)S(1)}, bf16[2,2,2,32,256]{4,3,2,1,0:T(8,128)(2,1)S(1)}, u32[]{:S(2)}, u32[]{:S(2)}) collective-permute-start(bf16[2,2,2,32,256]{4,3,2,1,0:T(8,128)(2,1)S(1)} %collective-permute-done.22.refs_12_), channel_id=1, source_target_pairs={{0,4},{4,0},{8,12},{12,8},{16,20},{20,16},{24,28},{28,24},{1,5},{5... | collective-permute-start | bytes 393224 | tf_op jit(solution)/shard_map/ppermute | solution.py:43
  165.8 16.5 %copy-start.23 = (bf16[2,2,2,32,256]{4,3,2,1,0:T(8,128)(2,1)}, bf16[2,2,2,32,256]{4,3,2,1,0:T(8,128)(2,1)S(1)}, u32[]{:S(2)}) copy-start(bf16[2,2,2,32,256]{4,3,2,1,0:T(8,128)(2,1)S(1)} %collective-permute-done.19.refs_9_) | copy-start | bytes 393220
  165.8 16.5 %collective-permute-start.12 = (bf16[2,2,2,32,256]{4,3,2,1,0:T(8,128)(2,1)S(1)}, bf16[2,2,2,32,256]{4,3,2,1,0:T(8,128)(2,1)S(1)}, u32[]{:S(2)}, u32[]{:S(2)}) collective-permute-start(bf16[2,2,2,32,256]{4,3,2,1,0:T(8,128)(2,1)S(1)} %collective-permute-done.11.refs_2_), channel_id=1, source_target_pairs={{0,4},{4,0},{8,12},{12,8},{16,20},{20,16},{24,28},{28,24},{1,5},{5... | collective-permute-start | bytes 393224 | tf_op jit(solution)/shard_map/ppermute | solution.py:43
  167.2 15.1 %copy-start.24 = (bf16[2,2,2,32,256]{4,3,2,1,0:T(8,128)(2,1)}, bf16[2,2,2,32,256]{4,3,2,1,0:T(8,128)(2,1)S(1)}, u32[]{:S(2)}) copy-start(bf16[2,2,2,32,256]{4,3,2,1,0:T(8,128)(2,1)S(1)} %collective-permute-done.15.refs_6_) | copy-start | bytes 393220
  167.2 15.2 %collective-permute-start.21 = (bf16[2,2,2,32,256]{4,3,2,1,0:T(8,128)(2,1)S(1)}, bf16[2,2,2,32,256]{4,3,2,1,0:T(8,128)(2,1)S(1)}, u32[]{:S(2)}, u32[]{:S(2)}) collective-permute-start(bf16[2,2,2,32,256]{4,3,2,1,0:T(8,128)(2,1)S(1)} %collective-permute-done.20.refs_10_), channel_id=1, source_target_pairs={{0,4},{4,0},{8,12},{12,8},{16,20},{20,16},{24,28},{28,24},{1,5},{5... | collective-permute-start | bytes 393224 | tf_op jit(solution)/shard_map/ppermute | solution.py:43
  168.3 14.0 %copy-start.25 = (bf16[2,2,2,32,256]{4,3,2,1,0:T(8,128)(2,1)}, bf16[2,2,2,32,256]{4,3,2,1,0:T(8,128)(2,1)S(1)}, u32[]{:S(2)}) copy-start(bf16[2,2,2,32,256]{4,3,2,1,0:T(8,128)(2,1)S(1)} %collective-permute-done.14.refs_5_) | copy-start | bytes 393220
  168.3 14.0 %collective-permute-start.16 = (bf16[2,2,2,32,256]{4,3,2,1,0:T(8,128)(2,1)S(1)}, bf16[2,2,2,32,256]{4,3,2,1,0:T(8,128)(2,1)S(1)}, u32[]{:S(2)}, u32[]{:S(2)}) collective-permute-start(bf16[2,2,2,32,256]{4,3,2,1,0:T(8,128)(2,1)S(1)} %collective-permute-done.15.refs_6_), channel_id=1, source_target_pairs={{0,4},{4,0},{8,12},{12,8},{16,20},{20,16},{24,28},{28,24},{1,5},{5... | collective-permute-start | bytes 393224 | tf_op jit(solution)/shard_map/ppermute | solution.py:43
  169.2 13.1 %copy-start.26 = (bf16[2,2,2,32,256]{4,3,2,1,0:T(8,128)(2,1)}, bf16[2,2,2,32,256]{4,3,2,1,0:T(8,128)(2,1)S(1)}, u32[]{:S(2)}) copy-start(bf16[2,2,2,32,256]{4,3,2,1,0:T(8,128)(2,1)S(1)} %collective-permute-done.24.refs_14_) | copy-start | bytes 393220
  169.2 13.2 %collective-permute-start.25 = (bf16[2,2,2,32,256]{4,3,2,1,0:T(8,128)(2,1)S(1)}, bf16[2,2,2,32,256]{4,3,2,1,0:T(8,128)(2,1)S(1)}, u32[]{:S(2)}, u32[]{:S(2)}) collective-permute-start(bf16[2,2,2,32,256]{4,3,2,1,0:T(8,128)(2,1)S(1)} %collective-permute-done.24.refs_14_), channel_id=1, source_target_pairs={{0,4},{4,0},{8,12},{12,8},{16,20},{20,16},{24,28},{28,24},{1,5},{5... | collective-permute-start | bytes 393224 | tf_op jit(solution)/shard_map/ppermute | solution.py:43
  182.3 0.7 copy-start.27
  182.4 0.7 copy-start.29
  182.4 0.7 copy-start.30
  (2 other events, 1.3 us)
where the time goes:
time: 196 us
  waiting for transfers between devices  88 us (45%)
  Pallas kernels  65.6 us (33%)
  starting transfers between devices  32 us (16%)
  local copies, waits for them, and re-layouts  7.67 us (4%)
    ppermute x34, waiting for transfers between devices, swap(): lax.ppermute(x, axis, [(s, s ^ bit) for s in range(lax.axis_size(axis))])  88 us
    ppermute x34, starting transfers between devices, swap(): lax.ppermute(x, axis, [(s, s ^ bit) for s in range(lax.axis_size(axis))])  32 us
    pallas_call x3, Pallas kernels, compress(): pl.pallas_call(functools.partial(compress_kernel, pieces=pieces, choices=...  31.3 us
    pallas_call x2, Pallas kernels, place(): pl.pallas_call(functools.partial(place_kernel, fronts=fronts, blocks=bloc...  23.6 us
    pallas_call x2, Pallas kernels, factor_columns(): pl.pallas_call(functools.partial(factor_kernel, first=first), in_specs=[S...  10.7 us
    unnamed x64, local copies, waits for them, and re-layouts  4.52 us
  transfers between devices with their start and end apart: 34, of which 11 were waited for; matrix products, arithmetic and copies ran while one was open for 2% of the time, Pallas kernels for 27%

commit v1 on v0

--- a/solution.py
+++ b/solution.py
@@ -52,35 +52,41 @@
     return bits
 
 
-def factor_kernel(meta, coupling, pivots, *refs, first):
-    *inverses, factor, scaled = refs
-    width = factor.shape[1]
-    total = None
-    for n, inverse in enumerate(inverses):
+def factor_kernel(meta, coupling, *refs, first, width, count, early, final):
+    total = refs[count][...] if early else None
+    for n, inverse in enumerate(refs[:count]):
         rows = inverse.shape[0]
         at = pl.multiple_of(meta[n] * rows, rows)
         lo = first if inverse.shape[1] > width else 0
         term = mm(coupling[:, pl.ds(at, rows)], inverse[:, lo:lo + width], NN)
         total = term if total is None else total + term
+    if not final:
+        refs[-1][...] = total
+        return
+    pivots, factor, scaled = refs[-3:]
     rounded = total.astype(jnp.bfloat16)
     factor[...] = rounded
     scaled[...] = (rounded.astype(jnp.float32) / pivots[:, first:first + width]).astype(jnp.bfloat16)
 
 
-def factor_columns(meta, coupling, pivots, inverses, first, width):
+def factor_columns(meta, coupling, inverses, first, width, early=None, pivots=None):
     rows = coupling.shape[0]
-    out = jax.ShapeDtypeStruct((rows, width), jnp.bfloat16)
+    final = pivots is not None
+    out = jax.ShapeDtypeStruct((rows, width), jnp.bfloat16 if final else jnp.float32)
+    operands = list(inverses) + ([early] if early is not None else []) + ([pivots] if final else [])
     return pl.pallas_call(
-        functools.partial(factor_kernel, first=first),
-        in_specs=[SMEM] + [VMEM] * (2 + len(inverses)),
-        out_specs=[VMEM, VMEM],
-        out_shape=[out, out],
+        functools.partial(
+            factor_kernel, first=first, width=width, count=len(inverses), early=early is not None, final=final
+        ),
+        in_specs=[SMEM] + [VMEM] * (1 + len(operands)),
+        out_specs=[VMEM, VMEM] if final else VMEM,
+        out_shape=[out, out] if final else out,
         compiler_params=pltpu.CompilerParams(vmem_limit_bytes=32 << 20),
         cost_estimate=pl.CostEstimate(
-            flops=2 * rows * coupling.shape[1] * out.shape[1], transcendentals=0, bytes_accessed=1 << 22
+            flops=2 * rows * sum(x.shape[0] for x in inverses) * width, transcendentals=0, bytes_accessed=1 << 22
         ),
         name="factor",
-    )(meta, coupling, pivots, *inverses)
+    )(meta, coupling, *operands)
 
 
 def compress_kernel(meta, *refs, pieces, choices):
@@ -197,6 +203,7 @@
     out = jax.ShapeDtypeStruct((2, tile_rows, total, rank, size), jnp.bfloat16)
     batch = total * tile_rows
     operands = [*scaled, trailing, omega]
+    count = len(operands)
     local = []
     for part, piece in zip(parts, pieces):
         operands += part[0]
@@ -223,7 +230,7 @@
             flops=8 * rows * width * total * size, transcendentals=0, bytes_accessed=8 * rows * width
         ),
         name="compress",
-    )(meta, *in_hbm(operands))
+    )(meta, *in_hbm(operands[:count]), *operands[count:])
 
 
 def place_kernel(meta, maps, base, *refs, fronts, blocks, row_dev):
@@ -255,7 +262,7 @@
 
     def selection(panel, child, t):
         lane = pl.multiple_of(panel * row_dev + t * size, size)
-        ids = maps[pl.ds(child, 1), pl.ds(lane, size)] - t * size
+        ids = maps[pl.ds(jnp.maximum(child, 0), 1), pl.ds(lane, size)] - t * size
         hit = lax.broadcasted_iota(jnp.int32, (size + spare, size), 0) == ids
         return jnp.where(hit, 1.0, 0.0).astype(jnp.bfloat16)
 
@@ -266,43 +273,42 @@
         load(step).start()
     left[...] = jnp.zeros(left.shape, left.dtype)
     right[...] = jnp.zeros(right.shape, right.dtype)
+    for slot in range(KIDS):
+        @pl.when(meta[slot] < 0)
+        def _():
+            for n in range(count):
+                mine[n][slot] = jnp.zeros(mine[n].shape[1:], jnp.bfloat16)
     for n in range(count):
         for slot in range(KIDS):
             fetch(n, slot, lambda copy: copy.wait())
     for slot in range(KIDS):
         lo = slot * depth
-
-        @pl.when(meta[slot] >= 0)
-        def _():
-            for i in range(tile_rows):
-                source = jnp.concatenate(
-                    [mine[n][slot, 0, i].reshape(blocks[n] * group, size) for n in range(count)], axis=0
+        for i in range(tile_rows):
+            source = jnp.concatenate(
+                [mine[n][slot, 0, i].reshape(blocks[n] * group, size) for n in range(count)], axis=0
+            )
+            spread = mm(selection(meta[2 * KIDS], meta[slot], i), source, NT).astype(jnp.bfloat16)
+            for step in range(steps):
+                left[step, i * size:(i + 1) * size + spare, lo + i * group:lo + (i + 1) * group] = (
+                    spread[:, step * group:(step + 1) * group]
                 )
-                spread = mm(selection(meta[2 * KIDS], meta[slot], i), source, NT).astype(jnp.bfloat16)
-                for step in range(steps):
-                    left[step, i * size:(i + 1) * size + spare, lo + i * group:lo + (i + 1) * group] = (
-                        spread[:, step * group:(step + 1) * group]
-                    )
 
     step = 0
     for n in range(count):
         for b in range(blocks[n]):
             for slot in range(KIDS):
                 lo = slot * depth
-
-                @pl.when(meta[slot] >= 0)
-                def _():
-                    for t in range(per_block):
-                        source = jnp.concatenate(
-                            [mine[n][slot, 1, i, b * per_block + t] for i in range(tile_rows)], axis=0
+                for t in range(per_block):
+                    source = jnp.concatenate(
+                        [mine[n][slot, 1, i, b * per_block + t] for i in range(tile_rows)], axis=0
+                    )
+                    pick = selection(meta[2 * KIDS + 1 + step], meta[slot], t)
+                    spread = mm(pick, source, NT).astype(jnp.bfloat16)
+                    for i in range(tile_rows):
+                        at = lo + i * group + t * rank
+                        right[t * size:(t + 1) * size + spare, at:at + rank] = (
+                            spread[:, i * rank:(i + 1) * rank]
                         )
-                        pick = selection(meta[2 * KIDS + 1 + step], meta[slot], t)
-                        spread = mm(pick, source, NT).astype(jnp.bfloat16)
-                        for i in range(tile_rows):
-                            at = lo + i * group + t * rank
-                            right[t * size:(t + 1) * size + spare, at:at + rank] = (
-                                spread[:, i * rank:(i + 1) * rank]
-                            )
 
             load(step).wait()
             lines[step] = (
@@ -344,7 +350,7 @@
             flops=8 * height * width * steps * depth, transcendentals=0, bytes_accessed=4 * height * width * steps
         ),
         name="place",
-    )(meta, extend_map, *in_hbm(operands))
+    )(meta, extend_map, *in_hbm(operands[:1]), *operands[1:])
 
 
 def spread_panels(x, lowest):
@@ -382,24 +388,25 @@
     offsets = range(panels)
     panel_of = jnp.stack([panel_here ^ offset for offset in offsets])
 
-    def columns(held, lo, hi):
+    def arrivals(held):
         parts = []
-        for offset in offsets:
-            if offset == 0:
-                parts.append(inverse)
-            elif offset == 1:
-                parts.append(near_inverse)
-            elif offset & 1:
+        for offset in offsets[2:]:
+            if offset & 1:
                 parts.append(swap(held[offset ^ 1], "panel", 1))
             else:
                 parts.append(held[offset])
-        return factor_columns(panel_of, rows_here, pivots, parts, lo, hi - lo)
-
-    factor_a, scaled_a = columns(held_a, 0, middle)
+        return parts
+
+    factor_a, scaled_a = factor_columns(
+        panel_of, rows_here, [inverse, near_inverse] + arrivals(held_a), 0, middle, pivots=pivots
+    )
     far_a = spread_panels(factor_a, 2)
     near_a = {offset ^ 1: swap(x, "panel", 1) for offset, x in far_a.items()}
     first = {**far_a, **near_a}
-    factor_b, scaled_b = columns(held_b, middle, width)
+    early = factor_columns(panel_of[:2], rows_here, [inverse, near_inverse], middle, width - middle)
+    factor_b, scaled_b = factor_columns(
+        panel_of[2:], rows_here, arrivals(held_b), middle, width - middle, early, pivots
+    )
     near_b = swap(factor_b, "panel", 1)
     scaled = (scaled_a, scaled_b)
 

time: 196 us -> 197 us (level); the launches traced: 196 us -> 194 us
  local copies, waits for them, and re-layouts: 7.67 us -> 14.2 us
  waiting for transfers between devices: 88 us -> 83.8 us
  Pallas kernels: 65.6 us -> 62.4 us
    unnamed x64 -> x32, local copies, waits for them, and re-layouts: 4.52 us -> 11 us
    ppermute x34, waiting for transfers between devices: 88 us -> 83.8 us  [swap(): lax.ppermute(x, axis, [(s, s ^ bit) for s in range(lax.axis_size(axis))])]
    pallas_call x2, Pallas kernels: 23.6 us -> 19.6 us  [place(): pl.pallas_call(functools.partial(place_kernel, fronts=fronts, blocks=bloc...]
    pallas_call x2 -> x3, Pallas kernels: 10.7 us -> 12 us  [factor_columns(): pl.pallas_call(functools.partial(factor_kernel, first=first, width=width,...]
  transfers between devices with their start and end apart: 34 -> 34, of which waited for: 11 -> 7; matrix products, arithmetic and copies ran while one was open for 2% -> 3% of each run, Pallas kernels for 27% -> 27%
where the time goes in v1:
time: 197 us; the launch traced here: 194 us
  waiting for transfers between devices  83.8 us (43%)
  Pallas kernels  62.4 us (32%)
  starting transfers between devices  30.7 us (16%)
  local copies, waits for them, and re-layouts  14.2 us (7%)
  other arithmetic  2.84 us (1%)
    ppermute x34, waiting for transfers between devices, swap(): lax.ppermute(x, axis, [(s, s ^ bit) for s in range(lax.axis_size(axis))])  83.8 us
    pallas_call x3, Pallas kernels, compress(): pl.pallas_call(functools.partial(compress_kernel, pieces=pieces, choices=...  30.8 us
    ppermute x34, starting transfers between devices, swap(): lax.ppermute(x, axis, [(s, s ^ bit) for s in range(lax.axis_size(axis))])  30.7 us
    pallas_call x2, Pallas kernels, place(): pl.pallas_call(functools.partial(place_kernel, fronts=fronts, blocks=bloc...  19.6 us
    pallas_call x3, Pallas kernels, factor_columns(): pl.pallas_call(functools.partial(factor_kernel, first=first, width=width,...  12 us
    unnamed x32, local copies, waits for them, and re-layouts  11 us
  transfers between devices with their start and end apart: 34, of which 7 were waited for; matrix products, arithmetic and copies ran while one was open for 3% of the time, Pallas kernels for 27%

profile of v1, /device:TPU:10, one launch (start us, length us, event | category | flops | bytes accessed | tf_op | source)
XLA Modules:
  0.0 194.4 jit_solution(12013313024029429498)
XLA Ops:
  0.0 1.4 slice.13
  1.5 1.6 collective-permute-start.3
  3.0 1.3 slice.12
  4.3 0.6 collective-permute-start.1
  4.9 22.7 %collective-permute-done.3.refs_0_ = bf16[512,1024]{1,0:T(8,128)(2,1)} collective-permute-done((bf16[512,1024]{1,0:T(8,128)(2,1)S(1)}, bf16[512,1024]{1,0:T(8,128)(2,1)}, u32[]{:S(2)}, u32[]{:S(2)}) %collective-permute-start.3) | collective-permute-done | bytes 1048608 | tf_op jit(solution)/shard_map/ppermute | solution.py:43
  27.7 21.8 %collective-permute-done.1.refs_2_ = bf16[512,1024]{1,0:T(8,128)(2,1)S(1)} collective-permute-done((bf16[512,1024]{1,0:T(8,128)(2,1)S(1)}, bf16[512,1024]{1,0:T(8,128)(2,1)S(1)}, u32[]{:S(2)}, u32[]{:S(2)}) %collective-permute-start.1) | collective-permute-done | bytes 1048608 | tf_op jit(solution)/shard_map/ppermute | solution.py:43
  49.6 1.6 copy-done.1
  51.2 2.9 %factor.4.refs_2_ = f32[512,1024]{1,0:T(8,128)S(1)} custom-call(s32[2]{0:T(128)S(1)} %pad_add_fusion.2.meta, bf16[512,2048]{1,0:T(8,128)(2,1)S(1)} %bitcast.25, bf16[512,2048]{1,0:T(8,128)(2,1)S(1)} %bitcast.31, bf16[512,2048]{1,0:T(8,128)(2,1)} %collective-permute-done.refs_1_), custom_call_target="tpu_custom_call" | custom-call | flops 1073741824 | bytes 4194304 | tf_op jit(solution)/shard_map/factor/pallas_call | solution.py:77
  54.1 4.0 %factor.5 = (bf16[512,1024]{1,0:T(8,128)(2,1)}, bf16[512,1024]{1,0:T(8,128)(2,1)S(1)}) custom-call(s32[2]{0:T(128)S(1)} %pad_add_fusion.1.meta, bf16[512,2048]{1,0:T(8,128)(2,1)S(1)} %bitcast.26, bf16[512,1024]{1,0:T(8,128)(2,1)} %collective-permute-done.3.refs_0_, bf16[512,1024]{1,0:T(8,128)(2,1)} %collective-permute-done.4.refs_1_, ...), custom_call_target="tpu_custom_call" | custom-call | flops 1073741824 | bytes 4194304 | tf_op jit(solution)/shard_map/factor/pallas_call | solution.py:77
  58.1 1.0 copy-done.4
  59.1 0.5 collective-permute-start.7
  59.6 5.2 %factor.3 = (bf16[512,1024]{1,0:T(8,128)(2,1)}, bf16[512,1024]{1,0:T(8,128)(2,1)S(1)}) custom-call(s32[4]{0:T(128)S(1)} %pad_add_fusion.meta, bf16[512,2048]{1,0:T(8,128)(2,1)S(1)} %bitcast.27, bf16[512,2048]{1,0:T(8,128)(2,1)S(1)} %bitcast.32, bf16[512,2048]{1,0:T(8,128)(2,1)} %collective-permute-done.refs_1_, ...), custom_call_target="tpu_custom_call" | custom-call | flops 2147483648 | bytes 4194304 | tf_op jit(solution)/shard_map/factor/pallas_call | solution.py:77
  64.8 1.0 copy-done.5
  65.8 1.5 collective-permute-start.5
  67.4 2.3 %broadcast_select_fusion = (bf16[256,1024]{1,0:T(8,128)(2,1)S(1)}, bf16[256,1024]{1,0:T(8,128)(2,1)}) fusion(pred[]{:T(512)S(6)} %eq.31, bf16[512,1024]{1,0:T(8,128)(2,1)} %collective-permute-done.7.refs_7_, s32[]{:T(128)S(6)} %select_n.26, bf16[512,1024]{1,0:T(8,128)(2,1)} %get-tuple-element.12.refs_6_, pred[]{:T(512)S(6)} %eq.30), kind=kLoop, calls=%fused_computation | loop fusion | flops 524288 | bytes 2097158 | tf_op jit(solution)/shard_map/jit(_where)/select_n | solution.py:434
  69.7 0.5 collective-permute-start.17
  70.2 1.5 collective-permute-start.8
  71.7 20.3 %collective-permute-done.5.refs_4_.refs_6_ = bf16[512,1024]{1,0:T(8,128)(2,1)S(1)} collective-permute-done((bf16[512,1024]{1,0:T(8,128)(2,1)}, bf16[512,1024]{1,0:T(8,128)(2,1)S(1)}, u32[]{:S(2)}, u32[]{:S(2)}) %collective-permute-start.5) | collective-permute-done | bytes 1048608 | tf_op jit(solution)/shard_map/ppermute | solution.py:43
  92.0 11.7 %compress.5.refs_0_ = bf16[2,2,4,32,256]{4,3,2,1,0:T(8,128)(2,1)S(1)} custom-call(s32[8]{0:T(128)S(1)} %stack.89.meta, bf16[512,1024]{1,0:T(8,128)(2,1)} %copy-done.5, bf16[512,1024]{1,0:T(8,128)(2,1)} %copy-done.4, f32[512,2048]{1,0:T(8,128)} %bitcast.35, f32[2,8,32,256]{3,2,1,0:T(8,128)} %bitcast.38, bf16[512,1024]{1,0:T(8,128)(2,1)} %get-tuple-element.11.refs_4_, ...), custom_call_target="tpu_custom_call" | custom-call | flops 8589934592 | bytes 8388608 | tf_op jit(solution)/shard_map/compress/pallas_call | solution.py:217
  103.8 2.6 %collective-permute-start.30 = (bf16[2,2,4,32,256]{4,3,2,1,0:T(8,128)(2,1)S(1)}, bf16[2,2,4,32,256]{4,3,2,1,0:T(8,128)(2,1)S(1)}, u32[]{:S(2)}, u32[]{:S(2)}) collective-permute-start(bf16[2,2,4,32,256]{4,3,2,1,0:T(8,128)(2,1)S(1)} %compress.5.refs_0_), channel_id=1, source_target_pairs={{0,16},{4,20},{8,24},{12,28},{16,0},{20,4},{24,8},{28,12},{1,17},{... | collective-permute-start | bytes 786440 | tf_op jit(solution)/shard_map/ppermute | solution.py:43
  106.4 0.2 collective-permute-start.18
  106.6 0.5 collective-permute-start.28
  107.1 11.1 %collective-permute-done.30.refs_4_ = bf16[2,2,4,32,256]{4,3,2,1,0:T(8,128)(2,1)S(1)} collective-permute-done((bf16[2,2,4,32,256]{4,3,2,1,0:T(8,128)(2,1)S(1)}, bf16[2,2,4,32,256]{4,3,2,1,0:T(8,128)(2,1)S(1)}, u32[]{:S(2)}, u32[]{:S(2)}) %collective-permute-start.30) | collective-permute-done | bytes 262176 | tf_op jit(solution)/shard_map/ppermute | solution.py:43
  118.2 1.4 collective-permute-start.32
  119.6 0.2 reduce-window.8
  119.8 0.1 stack.76.meta
  119.9 0.1 stack.86.meta
  120.1 0.6 collective-permute-start.27
  120.6 5.9 %collective-permute-done.32.refs_6_ = bf16[2,2,4,32,256]{4,3,2,1,0:T(8,128)(2,1)} collective-permute-done((bf16[2,2,4,32,256]{4,3,2,1,0:T(8,128)(2,1)S(1)}, bf16[2,2,4,32,256]{4,3,2,1,0:T(8,128)(2,1)}, u32[]{:S(2)}, u32[]{:S(2)}) %collective-permute-start.32) | collective-permute-done | bytes 262176 | tf_op jit(solution)/shard_map/ppermute | solution.py:43
  126.5 0.5 collective-permute-start.31
  127.1 1.5 collective-permute-start.29
  128.6 0.5 collective-permute-start.33
  129.1 9.5 %compress.4.refs_8_ = bf16[2,2,2,32,256]{4,3,2,1,0:T(8,128)(2,1)S(1)} custom-call(s32[8]{0:T(128)S(1)} %stack.86.meta, bf16[512,1024]{1,0:T(8,128)(2,1)} %copy-done.5, bf16[512,1024]{1,0:T(8,128)(2,1)} %copy-done.4, f32[512,2048]{1,0:T(8,128)} %bitcast.36, f32[2,8,32,256]{3,2,1,0:T(8,128)} %bitcast.39, ...), custom_call_target="tpu_custom_call" | custom-call | flops 4294967296 | bytes 8388608 | tf_op jit(solution)/shard_map/compress/pallas_call | solution.py:217
  138.7 3.4 %collective-permute-start.22 = (bf16[2,2,2,32,256]{4,3,2,1,0:T(8,128)(2,1)S(1)}, bf16[2,2,2,32,256]{4,3,2,1,0:T(8,128)(2,1)S(1)}, u32[]{:S(2)}, u32[]{:S(2)}) collective-permute-start(bf16[2,2,2,32,256]{4,3,2,1,0:T(8,128)(2,1)S(1)} %compress.4.refs_8_), channel_id=1, source_target_pairs={{0,16},{4,20},{8,24},{12,28},{16,0},{20,4},{24,8},{28,12},{1,17},{... | collective-permute-start | bytes 393224 | tf_op jit(solution)/shard_map/ppermute | solution.py:43
  142.1 9.5 %compress.3.refs_0_ = bf16[2,2,2,32,256]{4,3,2,1,0:T(8,128)(2,1)S(1)} custom-call(s32[8]{0:T(128)S(1)} %stack.76.meta, bf16[512,1024]{1,0:T(8,128)(2,1)} %copy-done.5, bf16[512,1024]{1,0:T(8,128)(2,1)} %copy-done.4, f32[512,2048]{1,0:T(8,128)} %bitcast.37, f32[2,8,32,256]{3,2,1,0:T(8,128)} %bitcast.40, ...), custom_call_target="tpu_custom_call" | custom-call | flops 4294967296 | bytes 8388608 | tf_op jit(solution)/shard_map/compress/pallas_call | solution.py:217
  151.7 0.7 copy-done.6
  152.4 0.3 collective-permute-start.20
  152.7 0.7 copy-done.8
  153.4 1.5 collective-permute-start.19
  154.9 0.7 copy-done.10
  155.6 0.2 collective-permute-start.13
  155.8 0.1 select_reduce_fusion
  155.9 0.7 copy-done.12
  156.7 1.5 collective-permute-start.11
  158.2 0.5 collective-permute-start.10
  158.8 0.6 collective-permute-start.24
  159.4 1.7 collective-permute-start.23
  161.1 1.7 collective-permute-done.13.refs_4_
  162.9 1.7 collective-permute-start.15
  164.6 0.1 concatenate.12.meta
  164.7 0.1 concatenate.11.meta
  164.7 1.1 collective-permute-start.14
  165.9 0.9 collective-permute-start.21
  166.8 0.2 collective-permute-done.24.refs_14_
  167.0 0.9 collective-permute-start.12
  167.9 1.1 collective-permute-start.25
  169.0 0.9 collective-permute-start.16
  169.9 0.9 copy-done.7
  170.9 0.9 copy-done.9
  171.8 0.9 copy-done.11
  172.8 0.9 copy-done.13
  173.7 0.8 copy-done.14
  174.6 9.0 %place.2.refs_16_ = bf16[1024,4096]{1,0:T(8,128)(2,1)} custom-call(s32[11]{0:T(128)S(1)} %concatenate.12.meta, s32[8,2048]{1,0:T(8,128)S(1)} %copy-done.14, bf16[1024,4096]{1,0:T(8,128)(2,1)} %bitcast.33, bf16[2,2,4,32,256]{4,3,2,1,0:T(8,128)(2,1)S(1)} %compress.5.refs_0_, bf16[2,2,4,32,256]{4,3,2,1,0:T(8,128)(2,1)S(1)} %copy-done.7, ...), custom_call_target="tpu_custom_call" | custom-call | flops 8589934592 | bytes 8388608 | tf_op jit(solution)/shard_map/place/pallas_call | solution.py:336
  183.6 10.6 %place.3 = bf16[1024,4096]{1,0:T(8,128)(2,1)} custom-call(s32[11]{0:T(128)S(1)} %concatenate.11.meta, s32[8,2048]{1,0:T(8,128)S(1)} %copy-done.14, bf16[1024,4096]{1,0:T(8,128)(2,1)} %bitcast.34, bf16[2,2,2,32,256]{4,3,2,1,0:T(8,128)(2,1)S(1)} %compress.3.refs_0_, ...), custom_call_target="tpu_custom_call", output_to_operand_aliasing={{}: (19, {})} | custom-call | flops 8589934592 | bytes 8388608 | tf_op jit(solution)/shard_map/place/pallas_call | solution.py:336
  (62 shorter events, 0.5 us)
Async XLA Ops:
  0.0 49.6 %copy-start = (bf16[1,512,2048]{2,1,0:T(8,128)(2,1)S(1)}, bf16[1,512,2048]{2,1,0:T(8,128)(2,1)}, u32[]{:S(2)}) copy-start(bf16[1,512,2048]{2,1,0:T(8,128)(2,1)} %param.8) | copy-start | bytes 6291460
  0.0 49.6 %collective-permute-start = (bf16[512,2048]{1,0:T(8,128)(2,1)}, bf16[512,2048]{1,0:T(8,128)(2,1)}, u32[]{:S(2)}, u32[]{:S(2)}) collective-permute-start(bf16[512,2048]{1,0:T(8,128)(2,1)} %bitcast.28), channel_id=1, source_target_pairs={{0,1},{1,0},{2,3},{3,2},{4,5},{5,4},{6,7},{7,6},{8,9},{9,8},{10,11... | collective-permute-start | bytes 6291464 | tf_op jit(solution)/shard_map/ppermute | solution.py:43
  1.5 26.2 %collective-permute-start.3 = (bf16[512,1024]{1,0:T(8,128)(2,1)S(1)}, bf16[512,1024]{1,0:T(8,128)(2,1)}, u32[]{:S(2)}, u32[]{:S(2)}) collective-permute-start(bf16[512,1024]{1,0:T(8,128)(2,1)S(1)} %slice.13), channel_id=1, source_target_pairs={{0,2},{1,3},{2,0},{3,1},{4,6},{5,7},{6,4},{7,5},{8,10},{9,11},{10,... | collective-permute-start | bytes 3145736 | tf_op jit(solution)/shard_map/ppermute | solution.py:43
  4.3 45.1 %collective-permute-start.1 = (bf16[512,1024]{1,0:T(8,128)(2,1)S(1)}, bf16[512,1024]{1,0:T(8,128)(2,1)S(1)}, u32[]{:S(2)}, u32[]{:S(2)}) collective-permute-start(bf16[512,1024]{1,0:T(8,128)(2,1)S(1)} %slice.12), channel_id=1, source_target_pairs={{0,2},{1,3},{2,0},{3,1},{4,6},{5,7},{6,4},{7,5},{8,10},{9,11},{10,... | collective-permute-start | bytes 3145736 | tf_op jit(solution)/shard_map/ppermute | solution.py:43
  27.7 26.5 %collective-permute-start.4 = (bf16[512,1024]{1,0:T(8,128)(2,1)}, bf16[512,1024]{1,0:T(8,128)(2,1)}, u32[]{:S(2)}, u32[]{:S(2)}) collective-permute-start(bf16[512,1024]{1,0:T(8,128)(2,1)} %collective-permute-done.3.refs_0_), channel_id=1, source_target_pairs={{0,1},{1,0},{2,3},{3,2},{4,5},{5,4},{6,7},{7,6},{8,9},{9,8},{10,11... | collective-permute-start | bytes 3145736 | tf_op jit(solution)/shard_map/ppermute | solution.py:43
  49.4 10.2 %collective-permute-start.2 = (bf16[512,1024]{1,0:T(8,128)(2,1)S(1)}, bf16[512,1024]{1,0:T(8,128)(2,1)}, u32[]{:S(2)}, u32[]{:S(2)}) collective-permute-start(bf16[512,1024]{1,0:T(8,128)(2,1)S(1)} %collective-permute-done.1.refs_2_), channel_id=1, source_target_pairs={{0,1},{1,0},{2,3},{3,2},{4,5},{5,4},{6,7},{7,6},{8,9},{9,8},{10,11... | collective-permute-start | bytes 3145736 | tf_op jit(solution)/shard_map/ppermute | solution.py:43
  49.6 1.6 copy-start.1
  51.2 2.9 %copy-start.3 = (f32[1,2048]{1,0:T(1,128)S(1)}, f32[1,2048]{1,0:T(1,128)}, u32[]{:S(2)}) copy-start(f32[1,2048]{1,0:T(1,128)} %refs_3_.1) | copy-start | bytes 24580
  54.1 5.5 %copy-start.2 = (bf16[1,512,2048]{2,1,0:T(8,128)(2,1)S(1)}, bf16[1,512,2048]{2,1,0:T(8,128)(2,1)}, u32[]{:S(2)}) copy-start(bf16[1,512,2048]{2,1,0:T(8,128)(2,1)} %param.9) | copy-start | bytes 6291460
  58.1 1.0 copy-start.4
  59.1 8.3 %collective-permute-start.7 = (bf16[512,1024]{1,0:T(8,128)(2,1)}, bf16[512,1024]{1,0:T(8,128)(2,1)}, u32[]{:S(2)}, u32[]{:S(2)}) collective-permute-start(bf16[512,1024]{1,0:T(8,128)(2,1)} %get-tuple-element.12.refs_6_), channel_id=1, source_target_pairs={{0,1},{1,0},{2,3},{3,2},{4,5},{5,4},{6,7},{7,6},{8,9},{9,8},{10,11... | collective-permute-start | bytes 3145736 | tf_op jit(solution)/shard_map/ppermute | solution.py:43
  64.8 1.0 copy-start.5
  65.8 26.2 %collective-permute-start.5 = (bf16[512,1024]{1,0:T(8,128)(2,1)}, bf16[512,1024]{1,0:T(8,128)(2,1)S(1)}, u32[]{:S(2)}, u32[]{:S(2)}) collective-permute-start(bf16[512,1024]{1,0:T(8,128)(2,1)} %get-tuple-element.11.refs_4_), channel_id=1, source_target_pairs={{0,2},{1,3},{2,0},{3,1},{4,6},{5,7},{6,4},{7,5},{8,10},{9,11},{10,... | collective-permute-start | bytes 3145736 | tf_op jit(solution)/shard_map/ppermute | solution.py:43
  67.3 24.7 %collective-permute-start.26 = (bf16[512,1024]{1,0:T(8,128)(2,1)}, bf16[512,1024]{1,0:T(8,128)(2,1)S(1)}, u32[]{:S(2)}, u32[]{:S(2)}) collective-permute-start(bf16[512,1024]{1,0:T(8,128)(2,1)} %get-tuple-element.11.refs_4_), channel_id=1, source_target_pairs={{0,1},{1,0},{2,3},{3,2},{4,5},{5,4},{6,7},{7,6},{8,9},{9,8},{10,11... | collective-permute-start | bytes 3145736 | tf_op jit(solution)/shard_map/ppermute | solution.py:43
  69.7 36.7 %collective-permute-start.17 = (bf16[256,1024]{1,0:T(8,128)(2,1)S(1)}, bf16[256,1024]{1,0:T(8,128)(2,1)}, u32[]{:S(2)}, u32[]{:S(2)}) collective-permute-start(bf16[256,1024]{1,0:T(8,128)(2,1)S(1)} %get-tuple-element.15), channel_id=1, source_target_pairs={{0,2},{1,3},{2,0},{3,1},{4,6},{5,7},{6,4},{7,5},{8,10},{9,11},{10,... | collective-permute-start | bytes 1572872 | tf_op jit(solution)/shard_map/ppermute | solution.py:43
  70.2 49.8 %collective-permute-start.8 = (bf16[256,1024]{1,0:T(8,128)(2,1)}, bf16[256,1024]{1,0:T(8,128)(2,1)}, u32[]{:S(2)}, u32[]{:S(2)}) collective-permute-start(bf16[256,1024]{1,0:T(8,128)(2,1)} %get-tuple-element.16), channel_id=1, source_target_pairs={{0,2},{1,3},{2,0},{3,1},{4,6},{5,7},{6,4},{7,5},{8,10},{9,11},{10,... | collective-permute-start | bytes 1572872 | tf_op jit(solution)/shard_map/ppermute | solution.py:43
  92.0 36.6 %collective-permute-start.6 = (bf16[512,1024]{1,0:T(8,128)(2,1)S(1)}, bf16[512,1024]{1,0:T(8,128)(2,1)S(1)}, u32[]{:S(2)}, u32[]{:S(2)}) collective-permute-start(bf16[512,1024]{1,0:T(8,128)(2,1)S(1)} %collective-permute-done.5.refs_4_.refs_6_), channel_id=1, source_target_pairs={{0,1},{1,0},{2,3},{3,2},{4,5},{5,4},{6,7},{7,6},{8,9},{9,8},{10,11... | collective-permute-start | bytes 3145736 | tf_op jit(solution)/shard_map/ppermute | solution.py:43
  92.0 27.6 %copy-start.15 = (s32[8]{0:T(128)S(1)}, s32[8]{0:T(128)}, u32[]{:S(2)}) copy-start(s32[8]{0:T(128)} %param.14) | copy-start | bytes 100
  103.8 14.4 %collective-permute-start.30 = (bf16[2,2,4,32,256]{4,3,2,1,0:T(8,128)(2,1)S(1)}, bf16[2,2,4,32,256]{4,3,2,1,0:T(8,128)(2,1)S(1)}, u32[]{:S(2)}, u32[]{:S(2)}) collective-permute-start(bf16[2,2,4,32,256]{4,3,2,1,0:T(8,128)(2,1)S(1)} %compress.5.refs_0_), channel_id=1, source_target_pairs={{0,16},{4,20},{8,24},{12,28},{16,0},{20,4},{24,8},{28,12},{1,17},{... | collective-permute-start | bytes 786440 | tf_op jit(solution)/shard_map/ppermute | solution.py:43
  106.4 20.7 %collective-permute-start.18 = (bf16[256,1024]{1,0:T(8,128)(2,1)}, bf16[256,1024]{1,0:T(8,128)(2,1)S(1)}, u32[]{:S(2)}, u32[]{:S(2)}) collective-permute-start(bf16[256,1024]{1,0:T(8,128)(2,1)} %collective-permute-done.17.refs_8_), channel_id=1, source_target_pairs={{0,1},{1,0},{2,3},{3,2},{4,5},{5,4},{6,7},{7,6},{8,9},{9,8},{10,11... | collective-permute-start | bytes 1572872 | tf_op jit(solution)/shard_map/ppermute | solution.py:43
  106.6 13.4 %collective-permute-start.28 = (bf16[2,2,4,32,256]{4,3,2,1,0:T(8,128)(2,1)S(1)}, bf16[2,2,4,32,256]{4,3,2,1,0:T(8,128)(2,1)S(1)}, u32[]{:S(2)}, u32[]{:S(2)}) collective-permute-start(bf16[2,2,4,32,256]{4,3,2,1,0:T(8,128)(2,1)S(1)} %compress.5.refs_0_), channel_id=1, source_target_pairs={{0,8},{4,12},{8,0},{12,4},{16,24},{20,28},{24,16},{28,20},{1,9},{5... | collective-permute-start | bytes 786440 | tf_op jit(solution)/shard_map/ppermute | solution.py:43
  118.2 8.4 %collective-permute-start.32 = (bf16[2,2,4,32,256]{4,3,2,1,0:T(8,128)(2,1)S(1)}, bf16[2,2,4,32,256]{4,3,2,1,0:T(8,128)(2,1)}, u32[]{:S(2)}, u32[]{:S(2)}) collective-permute-start(bf16[2,2,4,32,256]{4,3,2,1,0:T(8,128)(2,1)S(1)} %collective-permute-done.30.refs_4_), channel_id=1, source_target_pairs={{0,8},{4,12},{8,0},{12,4},{16,24},{20,28},{24,16},{28,20},{1,9},{5... | collective-permute-start | bytes 786440 | tf_op jit(solution)/shard_map/ppermute | solution.py:43
  120.0 18.7 %collective-permute-start.9 = (bf16[256,1024]{1,0:T(8,128)(2,1)}, bf16[256,1024]{1,0:T(8,128)(2,1)S(1)}, u32[]{:S(2)}, u32[]{:S(2)}) collective-permute-start(bf16[256,1024]{1,0:T(8,128)(2,1)} %collective-permute-done.8.refs_8_), channel_id=1, source_target_pairs={{0,1},{1,0},{2,3},{3,2},{4,5},{5,4},{6,7},{7,6},{8,9},{9,8},{10,11... | collective-permute-start | bytes 1572872 | tf_op jit(solution)/shard_map/ppermute | solution.py:43
  120.1 31.6 %collective-permute-start.27 = (bf16[2,2,4,32,256]{4,3,2,1,0:T(8,128)(2,1)S(1)}, bf16[2,2,4,32,256]{4,3,2,1,0:T(8,128)(2,1)S(1)}, u32[]{:S(2)}, u32[]{:S(2)}) collective-permute-start(bf16[2,2,4,32,256]{4,3,2,1,0:T(8,128)(2,1)S(1)} %compress.5.refs_0_), channel_id=1, source_target_pairs={{0,4},{4,0},{8,12},{12,8},{16,20},{20,16},{24,28},{28,24},{1,5},{5... | collective-permute-start | bytes 786440 | tf_op jit(solution)/shard_map/ppermute | solution.py:43
  126.5 26.1 %collective-permute-start.31 = (bf16[2,2,4,32,256]{4,3,2,1,0:T(8,128)(2,1)S(1)}, bf16[2,2,4,32,256]{4,3,2,1,0:T(8,128)(2,1)S(1)}, u32[]{:S(2)}, u32[]{:S(2)}) collective-permute-start(bf16[2,2,4,32,256]{4,3,2,1,0:T(8,128)(2,1)S(1)} %collective-permute-done.30.refs_4_), channel_id=1, source_target_pairs={{0,4},{4,0},{8,12},{12,8},{16,20},{20,16},{24,28},{28,24},{1,5},{5... | collective-permute-start | bytes 786440 | tf_op jit(solution)/shard_map/ppermute | solution.py:43
  127.1 27.8 %collective-permute-start.29 = (bf16[2,2,4,32,256]{4,3,2,1,0:T(8,128)(2,1)S(1)}, bf16[2,2,4,32,256]{4,3,2,1,0:T(8,128)(2,1)S(1)}, u32[]{:S(2)}, u32[]{:S(2)}) collective-permute-start(bf16[2,2,4,32,256]{4,3,2,1,0:T(8,128)(2,1)S(1)} %collective-permute-done.28.refs_2_), channel_id=1, source_target_pairs={{0,4},{4,0},{8,12},{12,8},{16,20},{20,16},{24,28},{28,24},{1,5},{5... | collective-permute-start | bytes 786440 | tf_op jit(solution)/shard_map/ppermute | solution.py:43
  128.6 27.4 %collective-permute-start.33 = (bf16[2,2,4,32,256]{4,3,2,1,0:T(8,128)(2,1)}, bf16[2,2,4,32,256]{4,3,2,1,0:T(8,128)(2,1)S(1)}, u32[]{:S(2)}, u32[]{:S(2)}) collective-permute-start(bf16[2,2,4,32,256]{4,3,2,1,0:T(8,128)(2,1)} %collective-permute-done.32.refs_6_), channel_id=1, source_target_pairs={{0,4},{4,0},{8,12},{12,8},{16,20},{20,16},{24,28},{28,24},{1,5},{5... | collective-permute-start | bytes 786440 | tf_op jit(solution)/shard_map/ppermute | solution.py:43
  138.7 19.5 %collective-permute-start.22 = (bf16[2,2,2,32,256]{4,3,2,1,0:T(8,128)(2,1)S(1)}, bf16[2,2,2,32,256]{4,3,2,1,0:T(8,128)(2,1)S(1)}, u32[]{:S(2)}, u32[]{:S(2)}) collective-permute-start(bf16[2,2,2,32,256]{4,3,2,1,0:T(8,128)(2,1)S(1)} %compress.4.refs_8_), channel_id=1, source_target_pairs={{0,16},{4,20},{8,24},{12,28},{16,0},{20,4},{24,8},{28,12},{1,17},{... | collective-permute-start | bytes 393224 | tf_op jit(solution)/shard_map/ppermute | solution.py:43
  151.7 0.7 copy-start.6
  152.4 6.4 %collective-permute-start.20 = (bf16[2,2,2,32,256]{4,3,2,1,0:T(8,128)(2,1)S(1)}, bf16[2,2,2,32,256]{4,3,2,1,0:T(8,128)(2,1)S(1)}, u32[]{:S(2)}, u32[]{:S(2)}) collective-permute-start(bf16[2,2,2,32,256]{4,3,2,1,0:T(8,128)(2,1)S(1)} %compress.4.refs_8_), channel_id=1, source_target_pairs={{0,8},{4,12},{8,0},{12,4},{16,24},{20,28},{24,16},{28,20},{1,9},{5... | collective-permute-start | bytes 393224 | tf_op jit(solution)/shard_map/ppermute | solution.py:43
  152.7 0.7 copy-start.8
  153.4 6.0 %collective-permute-start.19 = (bf16[2,2,2,32,256]{4,3,2,1,0:T(8,128)(2,1)S(1)}, bf16[2,2,2,32,256]{4,3,2,1,0:T(8,128)(2,1)S(1)}, u32[]{:S(2)}, u32[]{:S(2)}) collective-permute-start(bf16[2,2,2,32,256]{4,3,2,1,0:T(8,128)(2,1)S(1)} %compress.4.refs_8_), channel_id=1, source_target_pairs={{0,4},{4,0},{8,12},{12,8},{16,20},{20,16},{24,28},{28,24},{1,5},{5... | collective-permute-start | bytes 393224 | tf_op jit(solution)/shard_map/ppermute | solution.py:43
  154.9 0.7 copy-start.10
  155.6 7.3 %collective-permute-start.13 = (bf16[2,2,2,32,256]{4,3,2,1,0:T(8,128)(2,1)S(1)}, bf16[2,2,2,32,256]{4,3,2,1,0:T(8,128)(2,1)S(1)}, u32[]{:S(2)}, u32[]{:S(2)}) collective-permute-start(bf16[2,2,2,32,256]{4,3,2,1,0:T(8,128)(2,1)S(1)} %compress.3.refs_0_), channel_id=1, source_target_pairs={{0,16},{4,20},{8,24},{12,28},{16,0},{20,4},{24,8},{28,12},{1,17},{... | collective-permute-start | bytes 393224 | tf_op jit(solution)/shard_map/ppermute | solution.py:43
  155.9 0.7 copy-start.12
  156.7 8.1 %collective-permute-start.11 = (bf16[2,2,2,32,256]{4,3,2,1,0:T(8,128)(2,1)S(1)}, bf16[2,2,2,32,256]{4,3,2,1,0:T(8,128)(2,1)S(1)}, u32[]{:S(2)}, u32[]{:S(2)}) collective-permute-start(bf16[2,2,2,32,256]{4,3,2,1,0:T(8,128)(2,1)S(1)} %compress.3.refs_0_), channel_id=1, source_target_pairs={{0,8},{4,12},{8,0},{12,4},{16,24},{20,28},{24,16},{28,20},{1,9},{5... | collective-permute-start | bytes 393224 | tf_op jit(solution)/shard_map/ppermute | solution.py:43
  158.2 7.7 %collective-permute-start.10 = (bf16[2,2,2,32,256]{4,3,2,1,0:T(8,128)(2,1)S(1)}, bf16[2,2,2,32,256]{4,3,2,1,0:T(8,128)(2,1)S(1)}, u32[]{:S(2)}, u32[]{:S(2)}) collective-permute-start(bf16[2,2,2,32,256]{4,3,2,1,0:T(8,128)(2,1)S(1)} %compress.3.refs_0_), channel_id=1, source_target_pairs={{0,4},{4,0},{8,12},{12,8},{16,20},{20,16},{24,28},{28,24},{1,5},{5... | collective-permute-start | bytes 393224 | tf_op jit(solution)/shard_map/ppermute | solution.py:43
  158.8 8.2 %collective-permute-start.24 = (bf16[2,2,2,32,256]{4,3,2,1,0:T(8,128)(2,1)S(1)}, bf16[2,2,2,32,256]{4,3,2,1,0:T(8,128)(2,1)S(1)}, u32[]{:S(2)}, u32[]{:S(2)}) collective-permute-start(bf16[2,2,2,32,256]{4,3,2,1,0:T(8,128)(2,1)S(1)} %collective-permute-done.22.refs_12_), channel_id=1, source_target_pairs={{0,8},{4,12},{8,0},{12,4},{16,24},{20,28},{24,16},{28,20},{1,9},{5... | collective-permute-start | bytes 393224 | tf_op jit(solution)/shard_map/ppermute | solution.py:43
  159.4 8.5 %collective-permute-start.23 = (bf16[2,2,2,32,256]{4,3,2,1,0:T(8,128)(2,1)S(1)}, bf16[2,2,2,32,256]{4,3,2,1,0:T(8,128)(2,1)S(1)}, u32[]{:S(2)}, u32[]{:S(2)}) collective-permute-start(bf16[2,2,2,32,256]{4,3,2,1,0:T(8,128)(2,1)S(1)} %collective-permute-done.22.refs_12_), channel_id=1, source_target_pairs={{0,4},{4,0},{8,12},{12,8},{16,20},{20,16},{24,28},{28,24},{1,5},{5... | collective-permute-start | bytes 393224 | tf_op jit(solution)/shard_map/ppermute | solution.py:43
  162.9 6.1 %collective-permute-start.15 = (bf16[2,2,2,32,256]{4,3,2,1,0:T(8,128)(2,1)S(1)}, bf16[2,2,2,32,256]{4,3,2,1,0:T(8,128)(2,1)S(1)}, u32[]{:S(2)}, u32[]{:S(2)}) collective-permute-start(bf16[2,2,2,32,256]{4,3,2,1,0:T(8,128)(2,1)S(1)} %collective-permute-done.13.refs_4_), channel_id=1, source_target_pairs={{0,8},{4,12},{8,0},{12,4},{16,24},{20,28},{24,16},{28,20},{1,9},{5... | collective-permute-start | bytes 393224 | tf_op jit(solution)/shard_map/ppermute | solution.py:43
  164.7 18.9 %collective-permute-start.14 = (bf16[2,2,2,32,256]{4,3,2,1,0:T(8,128)(2,1)S(1)}, bf16[2,2,2,32,256]{4,3,2,1,0:T(8,128)(2,1)S(1)}, u32[]{:S(2)}, u32[]{:S(2)}) collective-permute-start(bf16[2,2,2,32,256]{4,3,2,1,0:T(8,128)(2,1)S(1)} %collective-permute-done.13.refs_4_), channel_id=1, source_target_pairs={{0,4},{4,0},{8,12},{12,8},{16,20},{20,16},{24,28},{28,24},{1,5},{5... | collective-permute-start | bytes 393224 | tf_op jit(solution)/shard_map/ppermute | solution.py:43
  165.9 17.7 %collective-permute-start.21 = (bf16[2,2,2,32,256]{4,3,2,1,0:T(8,128)(2,1)S(1)}, bf16[2,2,2,32,256]{4,3,2,1,0:T(8,128)(2,1)S(1)}, u32[]{:S(2)}, u32[]{:S(2)}) collective-permute-start(bf16[2,2,2,32,256]{4,3,2,1,0:T(8,128)(2,1)S(1)} %collective-permute-done.20.refs_10_), channel_id=1, source_target_pairs={{0,4},{4,0},{8,12},{12,8},{16,20},{20,16},{24,28},{28,24},{1,5},{5... | collective-permute-start | bytes 393224 | tf_op jit(solution)/shard_map/ppermute | solution.py:43
  167.0 16.6 %collective-permute-start.12 = (bf16[2,2,2,32,256]{4,3,2,1,0:T(8,128)(2,1)S(1)}, bf16[2,2,2,32,256]{4,3,2,1,0:T(8,128)(2,1)S(1)}, u32[]{:S(2)}, u32[]{:S(2)}) collective-permute-start(bf16[2,2,2,32,256]{4,3,2,1,0:T(8,128)(2,1)S(1)} %collective-permute-done.11.refs_2_), channel_id=1, source_target_pairs={{0,4},{4,0},{8,12},{12,8},{16,20},{20,16},{24,28},{28,24},{1,5},{5... | collective-permute-start | bytes 393224 | tf_op jit(solution)/shard_map/ppermute | solution.py:43
  167.9 15.7 %collective-permute-start.25 = (bf16[2,2,2,32,256]{4,3,2,1,0:T(8,128)(2,1)S(1)}, bf16[2,2,2,32,256]{4,3,2,1,0:T(8,128)(2,1)S(1)}, u32[]{:S(2)}, u32[]{:S(2)}) collective-permute-start(bf16[2,2,2,32,256]{4,3,2,1,0:T(8,128)(2,1)S(1)} %collective-permute-done.24.refs_14_), channel_id=1, source_target_pairs={{0,4},{4,0},{8,12},{12,8},{16,20},{20,16},{24,28},{28,24},{1,5},{5... | collective-permute-start | bytes 393224 | tf_op jit(solution)/shard_map/ppermute | solution.py:43
  169.0 14.6 %collective-permute-start.16 = (bf16[2,2,2,32,256]{4,3,2,1,0:T(8,128)(2,1)S(1)}, bf16[2,2,2,32,256]{4,3,2,1,0:T(8,128)(2,1)S(1)}, u32[]{:S(2)}, u32[]{:S(2)}) collective-permute-start(bf16[2,2,2,32,256]{4,3,2,1,0:T(8,128)(2,1)S(1)} %collective-permute-done.15.refs_6_), channel_id=1, source_target_pairs={{0,4},{4,0},{8,12},{12,8},{16,20},{20,16},{24,28},{28,24},{1,5},{5... | collective-permute-start | bytes 393224 | tf_op jit(solution)/shard_map/ppermute | solution.py:43
  169.9 0.9 copy-start.7
  170.9 0.9 copy-start.9
  171.8 0.9 copy-start.11
  172.8 0.9 copy-start.13
  173.7 0.8 copy-start.14
